TPU v7x, 512 devices: a whole 4x8x8 slice. The times are simulated.
512 devices in a mesh: dap: 32 (over x_lo, z, core), ch: 16 (over y, x_hi).
Axes of the slice: x: 4 (x_hi: 2, x_lo: 2; x = x_hi * 2 + x_lo), y: 8, z: 8, core: 2. Of those that a mesh axis runs over, the one named last changes fastest.
Arguments:
- pair_rep: bfloat16 [480, 480, 128], P('dap', 'ch'), may hold values from -400 to 400
- residue_mask: int32 [480], replicated, may hold values 0 or 1
- w_proj: bfloat16 [128, 512], replicated, may hold values from -0.5 to 0.5
- w_gate: bfloat16 [128, 128], replicated, may hold values from -0.5 to 0.5
- w_out: bfloat16 [128, 128], replicated, may hold values from -0.5 to 0.5
- cotangent: bfloat16 [480, 480, 128], P('dap', 'ch'), may hold values from -6 to 6
Outputs:
- pair_update: bfloat16 [480, 480, 128], P('dap', 'ch')
- grad_pair: bfloat16 [480, 480, 128], P('dap', 'ch')
Inputs may be any that keep to these rules, and one draw needn't show every extreme that they name: `residue_mask`: 1 marks a residue of the crop, 0 a padding position.
All inputs are finite; a program needn't handle non-finite values.
Results may differ from a plain program's by a relative error of at most 0.0085.
Values may be sent and summed in bfloat16 or wider, within the bound.
A program may use at most 64 MiB of HBM per device.

v0:
```python
import jax
import jax.numpy as jnp
from jax import lax
from jax.sharding import PartitionSpec as P

EPSILON = 1e-05


def laid_out(blocks, dim):
    blocks = jnp.moveaxis(blocks, 0, dim)
    shape = blocks.shape
    return blocks.reshape(*shape[:dim], shape[dim] * shape[dim + 1], *shape[dim + 2 :])


def piecewise(array, axis, dim, work, out_dim):
    extent = array.shape[dim]
    pieces = jnp.split(array, 2, axis=dim) if extent % 2 == 0 else [array]
    leading = jnp.arange(lax.axis_size(axis)) * extent
    blocks = [lax.all_gather(piece, axis) for piece in pieces]
    made = [jax.vmap(work)(b, leading + k * (extent // len(pieces))) for k, b in enumerate(blocks)]
    return laid_out(jnp.concatenate(made, axis=out_dim + 1), out_dim)


def side_by_side(arrays, axis, dim, along):
    ends, at = ([], 0)
    for a in arrays[:-1]:
        at += a.shape[along]
        ends.append(at)
    both = jnp.concatenate(arrays, axis=along)
    return tuple(jnp.split(lax.all_gather(both, axis, axis=dim, tiled=True), ends, axis=along))


def side_by_side_2(arrays, axis, split_dim, concat_dim, along):
    both = jnp.concatenate(arrays, axis=along)
    out, at, finished = (
        lax.all_to_all(both, axis, split_axis=split_dim, concat_axis=concat_dim, tiled=True),
        0,
        [],
    )
    for a in arrays:
        finished.append(lax.slice_in_dim(out, at, at + a.shape[along], axis=along))
        at += a.shape[along]
    return tuple(finished)


def normalize(values, axis):
    center = jnp.mean(values, axis=axis, keepdims=True)
    spread = values - center
    scale_inv = lax.rsqrt(jnp.mean(spread * spread, axis=axis, keepdims=True) + EPSILON)
    return (spread * scale_inv, scale_inv)


def norm_back(grad_in, normed, scale_inv, axis):
    first = jnp.mean(grad_in, axis=axis, keepdims=True)
    second = jnp.mean(grad_in * normed, axis=axis, keepdims=True)
    return scale_inv * (grad_in - first - normed * second)


def on_device(pair_rep, residue_mask, w_proj, w_gate, w_out, cotangent):
    row_count, columns, channels = pair_rep.shape
    hidden_width = w_out.shape[0]
    row_start = lax.axis_index("dap") * row_count
    col_start = lax.axis_index("ch") * columns
    live_flags = residue_mask.astype(jnp.float32)
    row_live = lax.dynamic_slice_in_dim(live_flags, row_start, row_count, 0)
    col_live = lax.dynamic_slice_in_dim(live_flags, col_start, columns, 0)
    cell_mask = row_live[:, None] * col_live[None, :]
    normed, pair_scale = normalize(pair_rep.astype(jnp.float32), 2)
    normed_half = normed.astype(jnp.bfloat16)
    projected = jnp.einsum("rkd,de->erk", normed_half, w_proj, preferred_element_type=jnp.float32)
    left_sig = jax.nn.sigmoid(projected[:hidden_width])
    left_val = projected[hidden_width : 2 * hidden_width]
    right_sig = jax.nn.sigmoid(projected[2 * hidden_width : 3 * hidden_width])
    right_val = projected[3 * hidden_width :]
    left_cells = (left_sig * left_val * cell_mask).astype(jnp.bfloat16)
    right_cells = (right_sig * right_val * cell_mask).astype(jnp.bfloat16)
    gate_values = jax.nn.sigmoid(
        jnp.einsum("rkd,de->rke", normed_half, w_gate, preferred_element_type=jnp.float32)
    )
    left_rows, right_rows = (
        lax.all_to_all(left_cells, "ch", split_axis=0, concat_axis=2, tiled=True),
        lax.all_to_all(right_cells, "ch", split_axis=0, concat_axis=2, tiled=True),
    )

    def row_block(shard_piece, offset):
        return jnp.einsum(
            "cik,cjk->cij", left_rows, shard_piece, preferred_element_type=jnp.float32
        )

    product = piecewise(right_rows, "dap", 1, row_block, 2).astype(jnp.bfloat16)
    product_cells = lax.all_to_all(product, "ch", split_axis=2, concat_axis=0, tiled=True)
    hidden_norm, hidden_scale = normalize(product_cells.astype(jnp.float32), 0)
    hidden_half = hidden_norm.astype(jnp.bfloat16)
    projected_out = jnp.einsum(
        "hrk,hd->rkd", hidden_half, w_out, preferred_element_type=jnp.float32
    )
    pair_update = (gate_values * projected_out).astype(jnp.bfloat16)
    upstream = cotangent.astype(jnp.float32)
    grad_out = (upstream * gate_values).astype(jnp.bfloat16)
    grad_logit = (upstream * projected_out * gate_values * (1.0 - gate_values)).astype(jnp.bfloat16)
    grad_hidden = jnp.einsum("rkd,hd->hrk", grad_out, w_out, preferred_element_type=jnp.float32)
    grad_product = norm_back(grad_hidden, hidden_norm, hidden_scale, 0).astype(jnp.bfloat16)
    grad_rows = lax.all_to_all(grad_product, "ch", split_axis=0, concat_axis=2, tiled=True)
    grad_cols = lax.all_to_all(grad_rows, "dap", split_axis=2, concat_axis=1, tiled=True)
    piece_left, piece_right = side_by_side((left_rows, right_rows), "dap", 1, 0)
    new_left = jnp.einsum(
        "cij,cjk->cik", grad_rows, piece_right, preferred_element_type=jnp.float32
    )
    new_right = jnp.einsum(
        "cij,cik->cjk", grad_cols, piece_left, preferred_element_type=jnp.float32
    )
    left_back, right_back = side_by_side_2(
        (new_left.astype(jnp.bfloat16), new_right.astype(jnp.bfloat16)), "ch", 2, 0, 1
    )
    masked_left = left_back.astype(jnp.float32) * cell_mask
    masked_right = right_back.astype(jnp.float32) * cell_mask
    grad_proj = jnp.concatenate(
        [
            masked_left * left_val * left_sig * (1.0 - left_sig),
            masked_left * left_sig,
            masked_right * right_val * right_sig * (1.0 - right_sig),
            masked_right * right_sig,
        ],
        axis=0,
    ).astype(jnp.bfloat16)
    grad_normed = jnp.einsum("erk,de->rkd", grad_proj, w_proj, preferred_element_type=jnp.float32)
    grad_normed = grad_normed + jnp.einsum(
        "rke,de->rkd", grad_logit, w_gate, preferred_element_type=jnp.float32
    )
    grad_pair = norm_back(grad_normed, normed, pair_scale, 2).astype(jnp.bfloat16)
    return (pair_update, grad_pair)


def solution(mesh):
    return jax.shard_map(
        on_device,
        mesh=mesh,
        in_specs=(P("dap", "ch", None), P(), P(), P(), P(), P("dap", "ch", None)),
        out_specs=(P("dap", "ch", None), P("dap", "ch", None)),
        check_vma=False,
    )
```

profile of v0, /device:TPU:1, one launch (start us, length us, event | category | flops | bytes accessed | tf_op | source)
XLA Modules:
  0.0 227.6 jit_solution(18086100395633365694)
XLA Ops:
  7.2 0.7 convert_element_type.75
  8.1 1.0 convert_reduce_fusion
  9.1 1.2 fusion.35
  10.4 1.2 convolution_bitcast_fusion
  11.8 0.5 copy.96
  12.2 0.9 reshape.88
  13.2 19.9 %all_to_all.99 = bf16[16,2,1800]{2,1,0:T(2,128)(2,1)S(1)} all-to-all(bf16[16,2,1800]{2,1,0:T(2,128)(2,1)S(1)} %reshape.88), channel_id=1, replica_groups=mesh['dap'=32,'ch'=16] {'ch'}, dimensions={0} | all-to-all | bytes 230400 | tf_op jit(solution)/shard_map/all_to_all | solution.py:82
  33.1 1.3 reshape.89
  34.7 1.1 all_gather.9
  35.9 0.5 copy.93
  36.4 1.6 reshape.90
  38.0 3.5 %all-to-all-start = ((bf16[16,2,1800]{2,1,0:T(2,128)(2,1)}), bf16[16,2,1800]{2,1,0:T(2,128)(2,1)S(1)}, u32[]{:S(2)}, u32[]{:S(2)}) async-start(bf16[16,2,1800]{2,1,0:T(2,128)(2,1)} %reshape.90), calls=%async_computation | async-start | bytes 245760 | tf_op jit(solution)/shard_map/all_to_all | solution.py:81
  41.7 0.5 all_to_all.84
  42.2 9.3 %all-to-all-done = bf16[16,2,1800]{2,1,0:T(2,128)(2,1)S(1)} async-done(((bf16[16,2,1800]{2,1,0:T(2,128)(2,1)}), bf16[16,2,1800]{2,1,0:T(2,128)(2,1)S(1)}, u32[]{:S(2)}, u32[]{:S(2)}) %all-to-all-start) | async-done | bytes 115232 | tf_op jit(solution)/shard_map/all_to_all | solution.py:81
  51.5 1.3 reshape.91
  53.1 0.5 all_to_all.75
  53.6 0.7 pad_maximum_fusion.1
  54.3 50.1 %all-gather.3.cloned.1.call-done = bf16[32,8,15,480]{3,1,2,0:T(8,128)(2,1)} async-done(((bf16[1,8,15,480]{3,1,2,0:T(8,128)(2,1)}), bf16[32,8,15,480]{3,1,2,0:T(8,128)(2,1)}) %all-gather.3.cloned.1.call-update) | async-done | bytes 3686416 | tf_op jit(solution)/shard_map/all_gather | solution.py:19
  104.5 4.7 %fusion.6 = bf16[8,15,32,15]{2,1,3,0:T(8,128)(2,1)S(1)} fusion(bf16[32,8,15,480]{3,1,2,0:T(8,128)(2,1)} %all-gather.3.cloned.1.call-done, bf16[8,15,480,1]{2,0,1,3:T(8,128)(2,1)S(1)} %bitcast.94), kind=kOutput, calls=%fused_computation.7 | convolution fusion | flops 55353600 | bytes 3916800 | tf_op jit(solution)/shard_map/vmap(cik,cjk->cij)/dot_general | solution.py:86
  109.2 0.9 copy.127
  110.0 1.1 reshape.92
  111.2 18.5 %all_to_all.100 = bf16[16,2,1800]{2,1,0:T(2,128)(2,1)S(1)} all-to-all(bf16[16,2,1800]{2,1,0:T(2,128)(2,1)S(1)} %reshape.92), channel_id=1, replica_groups=mesh['dap'=32,'ch'=16] {'ch'}, dimensions={0} | all-to-all | bytes 230400 | tf_op jit(solution)/shard_map/all_to_all | solution.py:91
  129.6 1.2 reshape.93
  130.9 0.8 copy.103
  131.7 0.6 reshape.82
  133.6 1.0 multiply_convert_fusion.5
  134.6 0.4 fusion.67
  135.3 0.5 copy.106
  135.7 0.9 reshape.94
  136.7 12.5 %all_to_all.101 = bf16[16,2,1800]{2,1,0:T(2,128)(2,1)S(1)} all-to-all(bf16[16,2,1800]{2,1,0:T(2,128)(2,1)S(1)} %reshape.94), channel_id=1, replica_groups=mesh['dap'=32,'ch'=16] {'ch'}, dimensions={0} | all-to-all | bytes 230400 | tf_op jit(solution)/shard_map/all_to_all | solution.py:103
  149.2 1.3 reshape.95
  150.8 0.5 all_to_all.83
  151.3 0.7 copy.112
  152.0 0.7 reshape.96
  152.7 19.6 %all_to_all.102 = bf16[32,2,900]{2,1,0:T(2,128)(2,1)S(1)} all-to-all(bf16[32,2,900]{2,1,0:T(2,128)(2,1)S(1)} %reshape.96), channel_id=1, replica_groups=mesh['dap'=32,'ch'=16] {'dap'}, dimensions={0} | all-to-all | bytes 230400 | tf_op jit(solution)/shard_map/all_to_all | solution.py:104
  172.3 0.9 reshape.97
  173.4 1.7 reshape.87
  175.1 7.2 %all-gather.5.cloned.1.call-done = bf16[16,480,480]{2,0,1:T(8,128)(2,1)} async-done(((bf16[16,15,480]{2,0,1:T(8,128)(2,1)}), bf16[16,480,480]{2,0,1:T(8,128)(2,1)}) %all-gather.5.cloned.1.call-update) | async-done | bytes 7372816 | tf_op jit(solution)/shard_map/all_gather | solution.py:30
  182.3 3.6 %fusion.68 = (bf16[8,480,480]{2,0,1:T(8,128)(2,1)S(1)}, bf16[8,480,480]{2,0,1:T(8,128)(2,1)S(1)}) fusion(bf16[16,480,480]{2,0,1:T(8,128)(2,1)} %all-gather.5.cloned.1.call-done), kind=kLoop, calls=%fused_computation.93 | loop fusion | bytes 14745600 | tf_op jit(solution)/shard_map/split | solution.py:30
  185.9 2.3 fusion.12
  188.1 2.2 fusion.15
  190.4 0.6 copy.117
  191.0 1.3 reshape.98
  192.3 21.2 %all_to_all.103 = bf16[16,2,3600]{2,1,0:T(2,128)(2,1)S(1)} all-to-all(bf16[16,2,3600]{2,1,0:T(2,128)(2,1)S(1)} %reshape.98), channel_id=1, replica_groups=mesh['dap'=32,'ch'=16] {'ch'}, dimensions={0} | all-to-all | bytes 460800 | tf_op jit(solution)/shard_map/all_to_all | solution.py:36
  213.5 1.3 reshape.99
  214.8 2.3 %copy.119 = bf16[16,8,30,30]{3,1,0,2:T(8,128)(2,1)S(1)} copy(bf16[16,8,30,30]{2,1,3,0:T(8,128)(2,1)S(1)} %bitcast.88) | data formatting | bytes 460800 | tf_op jit(solution)/shard_map/all_to_all | solution.py:36
  218.3 1.4 fusion.66
  219.8 1.0 fusion.34
  (47 shorter events, 4.7 us)
Async XLA Ops:
  7.2 3.2 %copy-start = (bf16[128,512]{1,0:T(8,128)(2,1)S(1)}, bf16[128,512]{1,0:T(8,128)(2,1)}, u32[]{:S(2)}) copy-start(bf16[128,512]{1,0:T(8,128)(2,1)} %param.8) | copy-start | bytes 393220
  7.2 97.3 %all-gather.3.cloned.1.call-start = ((), (), s32[]{:S(2)}) async-start(), calls=%async_computation.6 | async-start | bytes 4055040 | tf_op jit(solution)/shard_map/all_gather | solution.py:19
  38.0 13.5 %all-to-all-start = ((bf16[16,2,1800]{2,1,0:T(2,128)(2,1)}), bf16[16,2,1800]{2,1,0:T(2,128)(2,1)S(1)}, u32[]{:S(2)}, u32[]{:S(2)}) async-start(bf16[16,2,1800]{2,1,0:T(2,128)(2,1)} %reshape.90), calls=%async_computation | async-start | bytes 245760 | tf_op jit(solution)/shard_map/all_to_all | solution.py:81
  41.5 140.8 %all-gather.5.cloned.1.call-start = ((), (), s32[]{:S(2)}) async-start(), calls=%async_computation.7 | async-start | bytes 8110080 | tf_op jit(solution)/shard_map/all_gather | solution.py:30
  130.9 2.4 %copy-start.6 = (bf16[128,128]{1,0:T(8,128)(2,1)S(1)}, bf16[128,128]{1,0:T(8,128)(2,1)}, u32[]{:S(2)}) copy-start(bf16[128,128]{1,0:T(8,128)(2,1)} %param.10) | copy-start | bytes 98308
  130.9 2.7 %copy-start.1 = (bf16[15,30,128]{2,1,0:T(8,128)(2,1)S(1)}, bf16[15,30,128]{2,1,0:T(8,128)(2,1)}, u32[]{:S(2)}) copy-start(bf16[15,30,128]{2,1,0:T(8,128)(2,1)} %param.6) | copy-start | bytes 345604
  130.9 2.7 %copy-start.7 = (bf16[128,128]{1,0:T(8,128)(2,1)S(1)}, bf16[128,128]{1,0:T(8,128)(2,1)}, u32[]{:S(2)}) copy-start(bf16[128,128]{1,0:T(8,128)(2,1)} %param.9) | copy-start | bytes 98308
  133.0 1.6 copy-start.5
  133.6 39.7 %copy-start.4 = (f32[15,30,128]{2,1,0:T(8,128)}, f32[15,30,128]{2,1,0:T(8,128)S(1)}, u32[]{:S(2)}) copy-start(f32[15,30,128]{2,1,0:T(8,128)S(1)} %fusion.51) | copy-start | bytes 691204
  134.6 37.7 %copy-start.2 = (f32[15,30,128]{2,1,0:T(8,128)}, f32[15,30,128]{2,1,0:T(8,128)S(1)}, u32[]{:S(2)}) copy-start(f32[15,30,128]{2,1,0:T(8,128)S(1)} %get-tuple-element.19) | copy-start | bytes 691204
  217.2 1.2 copy-start.3
Sparse Core Ops, SparseCore 0:
  36.0 68.4 all-gather.2
  106.6 75.6 all-gather.4
where the time goes:
time: 228 us
  blocking collectives  91.7 us (40%)
  waiting for transfers between devices  66.6 us (29%)
  local copies, waits for them, and re-layouts  31.7 us (14%)
  between operations  14.4 us (6%)
  matrix products  13.7 us (6%)
  other arithmetic  5.73 us (3%)
  starting transfers between devices  3.77 us (2%)
    all_gather x1, waiting for transfers between devices, piecewise(): blocks = [lax.all_gather(piece, axis) for piece in pieces]  50.1 us
    all_to_all x1, blocking collectives, side_by_side_2(): lax.all_to_all(both, axis, split_axis=split_dim, concat_axis=concat_dim,...  21.2 us
    all_to_all x1, blocking collectives, on_device(): lax.all_to_all(right_cells, 'ch', split_axis=0, concat_axis=2, tiled=True)  19.9 us
    all_to_all x1, blocking collectives, on_device(): lax.all_to_all(grad_rows, 'dap', split_axis=2, concat_axis=1, tiled=True)  19.6 us
    all_to_all x1, blocking collectives, on_device(): lax.all_to_all(product, 'ch', split_axis=2, concat_axis=0, tiled=True)  18.5 us
    unnamed x30, local copies, waits for them, and re-layouts  14.6 us
    all_to_all x1, blocking collectives, on_device(): lax.all_to_all(grad_product, 'ch', split_axis=0, concat_axis=2, tiled=True)  12.5 us
    all_to_all x1, waiting for transfers between devices, on_device(): lax.all_to_all(left_cells, 'ch', split_axis=0, concat_axis=2, tiled=True)  9.3 us
  transfers between devices with their start and end apart: 3, of which 3 were waited for; matrix products, arithmetic and copies ran while one was open for 10% of the time, Pallas kernels for 0%

commit v1 on v0

v1 whole, which is shorter than its diff:
```python
import functools

import jax
import jax.numpy as jnp
from jax import lax
from jax.experimental import pallas as pl
from jax.experimental.pallas import tpu as pltpu
from jax.sharding import PartitionSpec as P

EPSILON = 1e-05
F32 = jnp.float32
BF16 = jnp.bfloat16
GROUP = 8
CELLS = 512


def owner_of(channel, dap_size):
    if dap_size == 32:
        return lax.rem(channel, 2) * 16 + 2 * channel + 1
    return channel


def owned_by(me, dap_size):
    if dap_size == 32:
        z = lax.rem(me // 2, 8)
        return z, jnp.logical_and(lax.rem(me, 2) == 1, me // 16 == lax.rem(z, 2))
    return me, me < GROUP


def dot(a, b, contract):
    return lax.dot_general(a, b, (contract, ((), ())), preferred_element_type=F32)


def swap_blocks(rows):
    block = lax.broadcasted_iota(jnp.int32, rows[0].shape, 1) // 32
    odd = lax.rem(block, 2) == 1
    high = block >= 2
    x0, x1, x2, x3 = rows
    z0 = jnp.where(odd, pltpu.roll(x1, 32, 1), x0)
    z1 = jnp.where(odd, x1, pltpu.roll(x0, 96, 1))
    z2 = jnp.where(odd, pltpu.roll(x3, 32, 1), x2)
    z3 = jnp.where(odd, x3, pltpu.roll(x2, 96, 1))
    return (
        jnp.where(high, pltpu.roll(z2, 64, 1), z0),
        jnp.where(high, pltpu.roll(z3, 64, 1), z1),
        jnp.where(high, z2, pltpu.roll(z0, 64, 1)),
        jnp.where(high, z3, pltpu.roll(z1, 64, 1)),
    )


def cells_to_rows(cells, mid, rows):
    for t in range(cells.shape[0] // 4):
        for q in range(4):
            lanes = pl.ds(q * 128, 128)
            moved = swap_blocks([cells[4 * t + a, :, lanes].astype(F32) for a in range(4)])
            for b in range(4):
                mid[t, pl.ds(4 * q + b, GROUP, stride=16), :] = moved[b]
    for t in range(cells.shape[0] // 4):
        for m in range(GROUP):
            rows[m, :, pl.ds(t * 128, 128)] = mid[t, pl.ds(16 * m, 16), :].astype(BF16)


def rows_to_cells(rows, mid, cells):
    for t in range(cells.shape[0] // 4):
        for m in range(GROUP):
            mid[t, pl.ds(16 * m, 16), :] = rows[m, :, pl.ds(t * 128, 128)].astype(F32)
    for t in range(cells.shape[0] // 4):
        for q in range(4):
            lanes = pl.ds(q * 128, 128)
            moved = swap_blocks([mid[t, pl.ds(4 * q + b, GROUP, stride=16), :] for b in range(4)])
            for a in range(4):
                cells[4 * t + a, :, lanes] = moved[a].astype(BF16)


def kernel(
    nd,
    ns,
    x_ref,
    cot_ref,
    mask_ref,
    wp_ref,
    wg_ref,
    wo_ref,
    upd_ref,
    gpair_ref,
    padded,
    live,
    proj,
    normed,
    gate,
    cot,
    ghid,
    glogit,
    mid,
    out1,
    in1,
    out2,
    in2,
    own_in,
    own_out,
    send_sem,
    recv_sem,
):
    rows, columns, chans = x_ref.shape
    half = columns // 2
    hidden = ns * GROUP
    me_d = lax.axis_index("dap")
    me_s = lax.axis_index("ch")
    my_m, is_owner = owned_by(me_d, nd)

    barrier = pltpu.get_barrier_semaphore()

    def greet(peer):
        pl.semaphore_signal(
            barrier, inc=1, device_id=peer, device_id_type=pl.DeviceIdType.MESH
        )

    @pl.loop(1, ns)
    def _(r):
        greet({"ch": lax.rem(me_s + r, ns)})

    @pl.when(is_owner)
    def _():
        @pl.loop(1, nd)
        def _(r):
            greet({"dap": lax.rem(me_d + r, nd)})

    @pl.when(jnp.logical_not(is_owner))
    def _():
        @pl.loop(0, GROUP)
        def _(m):
            greet({"dap": owner_of(m, nd)})

    def push(src, dst, sem, peer):
        return pltpu.make_async_remote_copy(
            src_ref=src,
            dst_ref=dst,
            send_sem=send_sem.at[sem],
            recv_sem=recv_sem.at[sem],
            device_id=peer,
            device_id_type=pl.DeviceIdType.MESH,
        )

    def across_ch(src, dst, sem):
        @pl.loop(1, ns)
        def _(r):
            peer = lax.rem(me_s + r, ns)
            push(src.at[peer], dst.at[me_s], sem, {"ch": peer}).start()

        dst[me_s] = src[me_s]

    def await_ch(dst, sem):
        some = dst.at[pl.ds(0, ns - 1)]
        push(some, some, sem, {"ch": me_s}).wait_recv()

    def to_owners(src, dst, sem):
        @pl.loop(0, GROUP)
        def _(r):
            m = lax.rem(my_m + r, GROUP)
            owner = owner_of(m, nd)

            @pl.when(owner != me_d)
            def _():
                push(src.at[m], dst.at[me_d], sem, {"dap": owner}).start()

            @pl.when(owner == me_d)
            def _():
                dst[me_d] = src[m]

    def await_owner(dst, sem):
        some = dst.at[pl.ds(0, nd - 1)]
        push(some, some, sem, {"dap": me_d}).wait_recv()

    def from_owner(src, dst, sem, d):
        @pl.when(d != me_d)
        def _():
            push(src.at[d], dst.at[my_m], sem, {"dap": d}).start()

        @pl.when(d == me_d)
        def _():
            dst[my_m] = src[d]

    def await_rows(dst, sem):
        @pl.when(is_owner)
        def _():
            some = dst.at[pl.ds(0, GROUP - 1)]
            push(some, some, sem, {"dap": me_d}).wait_recv()

        @pl.when(jnp.logical_not(is_owner))
        def _():
            push(dst, dst, sem, {"dap": me_d}).wait_recv()

    lane = lax.broadcasted_iota(jnp.int32, (1, CELLS), 1)
    place = lax.rem(lane, 16)
    used = jnp.logical_and(place < half, lane < rows * 32)
    first_half = lax.rem(lane, 32) < 16

    eye = (
        lax.broadcasted_iota(jnp.int32, (chans, chans), 0)
        == lax.broadcasted_iota(jnp.int32, (chans, chans), 1)
    ).astype(F32).astype(BF16)

    def cells_first(ref, slot):
        padded[slot] = jnp.zeros(padded.shape[1:], BF16)
        padded[slot, 0:rows, 0:columns, :] = ref[...]
        flat = padded[slot].reshape(CELLS, chans)
        turned = dot(eye, flat, ((1,), (1,)))
        spread = jnp.where(first_half, turned, pltpu.roll(turned, 1, 1))
        return jnp.where(used, spread, 0.0)

    def cells_last(turned):
        closed = jnp.where(
            lax.rem(lane, 32) < half, turned, pltpu.roll(turned, CELLS - 1, 1)
        )
        return closed.T.reshape(16, 32, chans)[0:rows, 0:columns, :].astype(BF16)

    xt = cells_first(x_ref, 0)
    center = jnp.mean(xt, axis=0, keepdims=True)
    spread = xt - center
    pair_scale = lax.rsqrt(jnp.mean(spread * spread, axis=0, keepdims=True) + EPSILON)
    nt = spread * pair_scale
    normed[...] = nt
    nh = nt.astype(BF16)

    residues = mask_ref.shape[1]
    total = nd * 16
    live[...] = jnp.zeros(live.shape, F32)
    live[:, 0:residues] = jnp.broadcast_to(mask_ref[...].astype(F32), (8, residues))
    flags = live[...].astype(BF16)

    def one_hot(hot):
        return jnp.where(hot, 1.0, 0.0).astype(BF16)

    at = lax.broadcasted_iota(jnp.int32, (total, 128), 0)
    lane_1 = lax.broadcasted_iota(jnp.int32, (total, 128), 1)
    row_flags = dot(
        flags, one_hot(jnp.logical_and(at == rows * me_d + lane_1, lane_1 < rows)), ((1,), (0,))
    )
    col_at = columns * me_s + half * (lax.rem(lane_1, 32) // 16) + lax.rem(lane_1, 16)
    col_flags = dot(
        flags, one_hot(jnp.logical_and(at == col_at, lax.rem(lane_1, 16) < half)), ((1,), (0,))
    )
    spot = lax.broadcasted_iota(jnp.int32, (128, CELLS), 0)
    row_of = lax.broadcasted_iota(jnp.int32, (128, CELLS), 1) // 32
    row_mask = dot(row_flags.astype(BF16), one_hot(spot == row_of), ((1,), (0,)))
    col_mask = jnp.concatenate([col_flags] * (CELLS // 128), axis=1)
    mask = (row_mask * col_mask)[0:1]

    def project(part):
        raw = dot(wp_ref[:, pl.ds(part * hidden, hidden)], nh, ((0,), (0,)))
        return raw

    def edge(part, slot):
        sig = jax.nn.sigmoid(project(part))
        val = project(part + 1)
        proj[part] = sig
        proj[part + 1] = val
        out1[slot] = (sig * val * mask).reshape(ns, GROUP, CELLS).astype(BF16)

    edge(0, 0)
    pl.semaphore_wait(barrier, ns - 1 + jnp.where(is_owner, nd - 1, GROUP))
    across_ch(out1.at[0], in1.at[0], 0)
    edge(2, 1)
    across_ch(out1.at[1], in1.at[1], 1)

    gv = jax.nn.sigmoid(dot(wg_ref[...], nh, ((0,), (0,))))
    gate[...] = gv
    ct = cells_first(cot_ref, 1)
    cot[...] = ct
    gh = dot(wo_ref[...], (ct * gv).astype(BF16), ((1,), (0,)))
    ghid[...] = gh - jnp.mean(gh, axis=0, keepdims=True)

    for a in range(2):
        await_ch(in1.at[a], a)
        cells_to_rows(in1.at[a], mid, out2.at[a])
        to_owners(out2.at[a], own_in.at[a], 2 + a)

    width = ns * 32
    per = 128 // 16

    def all_rows(ref):
        return ref[...].reshape(nd * 16, width)

    def return_rows(buffer, back, sem, b, value):
        own_out[buffer, pl.ds(per * b, per)] = value.astype(BF16).reshape(per, 16, width)

        @pl.loop(0, per)
        def _(e):
            from_owner(own_out.at[buffer], in2.at[back], sem, per * b + e)

    @pl.when(is_owner)
    def _():
        await_owner(own_in.at[0], 2)
        await_owner(own_in.at[1], 3)

        @pl.loop(0, nd // per)
        def _(b):
            left = own_in[0, pl.ds(per * b, per)].reshape(128, width)
            return_rows(0, 0, 4, b, dot(left, all_rows(own_in.at[1]), ((1,), (1,))))

    await_rows(in2.at[0], 4)
    rows_to_cells(in2.at[0], mid, out1.at[2])
    across_ch(out1.at[2], in1.at[2], 5)
    await_ch(in1.at[2], 5)

    prod = in1[2].reshape(hidden, CELLS).astype(F32)
    away = prod - jnp.mean(prod, axis=0, keepdims=True)
    hidden_scale = lax.rsqrt(jnp.mean(away * away, axis=0, keepdims=True) + EPSILON)
    hn = away * hidden_scale
    gh_away = ghid[...]
    second = jnp.mean((gh_away) * hn, axis=0, keepdims=True)
    gprod = hidden_scale * (gh_away - hn * second)
    out1[3] = gprod.reshape(ns, GROUP, CELLS).astype(BF16)
    across_ch(out1.at[3], in1.at[3], 6)

    po = dot(wo_ref[...], hn.astype(BF16), ((0,), (0,)))
    gv = gate[...]
    glogit[...] = (cot[...] * po * gv * (1.0 - gv)).astype(BF16)
    upd_ref[...] = cells_last(gv * po)

    await_ch(in1.at[3], 6)
    cells_to_rows(in1.at[3], mid, out2.at[2])
    to_owners(out2.at[2], own_in.at[2], 7)

    @pl.when(is_owner)
    def _():
        await_owner(own_in.at[2], 7)

        @pl.loop(0, nd // per)
        def _(b):
            part = own_in[2, pl.ds(per * b, per)].reshape(128, width)
            return_rows(1, 1, 8, b, dot(part, all_rows(own_in.at[1]), ((1,), (0,))))

        @pl.loop(0, nd // per)
        def _(b):
            lanes = pl.ds(pl.multiple_of(b * 128, 128), 128)
            part = own_in[2, :, :, lanes].reshape(nd * 16, 128)
            return_rows(2, 2, 9, b, dot(part, all_rows(own_in.at[0]), ((0,), (0,))))

    base = dot(wg_ref[...], glogit[...], ((1,), (0,)))

    for a in range(2):
        await_rows(in2.at[1 + a], 8 + a)
        rows_to_cells(in2.at[1 + a], mid, out1.at[4 + a])
        across_ch(out1.at[4 + a], in1.at[4 + a], 10 + a)

    for a in range(2):
        await_ch(in1.at[4 + a], 10 + a)
        masked = in1[4 + a].reshape(hidden, CELLS).astype(F32) * mask
        sig = proj[2 * a]
        val = proj[2 * a + 1]
        to_sig = (masked * val * sig * (1.0 - sig)).astype(BF16)
        to_val = (masked * sig).astype(BF16)
        base = base + dot(wp_ref[:, pl.ds(2 * a * hidden, hidden)], to_sig, ((1,), (0,)))
        base = base + dot(wp_ref[:, pl.ds((2 * a + 1) * hidden, hidden)], to_val, ((1,), (0,)))

    nt = normed[...]
    first = jnp.mean(base, axis=0, keepdims=True)
    second = jnp.mean(base * nt, axis=0, keepdims=True)
    gpair_ref[...] = cells_last(pair_scale * (base - first - nt * second))

    def sent(ref, sem):
        push(ref, ref, sem, {"ch": me_s}).wait_send()

    few = pl.ds(0, ns - 1)
    for buffer, sem in ((0, 0), (1, 1), (2, 5), (3, 6), (4, 10), (5, 11)):
        sent(out1.at[buffer, few], sem)
    for buffer, sem in ((0, 2), (1, 3), (2, 7)):

        @pl.when(is_owner)
        def _():
            sent(out2.at[buffer, pl.ds(0, GROUP - 1)], sem)

        @pl.when(jnp.logical_not(is_owner))
        def _():
            sent(out2.at[buffer], sem)

    @pl.when(is_owner)
    def _():
        for buffer, sem in ((0, 4), (1, 8), (2, 9)):
            sent(own_out.at[buffer, pl.ds(0, nd - 1)], sem)


def on_device(nd, ns, pair_rep, residue_mask, w_proj, w_gate, w_out, cotangent):
    hidden, chans = w_out.shape
    vmem = pl.BlockSpec(memory_space=pltpu.VMEM)
    shape = jax.ShapeDtypeStruct(pair_rep.shape, BF16)
    width = ns * 32
    return pl.pallas_call(
        functools.partial(kernel, nd, ns),
        out_shape=(shape, shape),
        in_specs=[vmem] * 6,
        out_specs=(vmem, vmem),
        scratch_shapes=[
            pltpu.VMEM((2, 16, 32, chans), BF16),
            pltpu.VMEM((8, nd * 16), F32),
            pltpu.VMEM((4, hidden, CELLS), F32),
            pltpu.VMEM((chans, CELLS), F32),
            pltpu.VMEM((chans, CELLS), F32),
            pltpu.VMEM((chans, CELLS), F32),
            pltpu.VMEM((hidden, CELLS), F32),
            pltpu.VMEM((chans, CELLS), BF16),
            pltpu.VMEM((ns // 4, 16 * GROUP, 128), F32),
            pltpu.VMEM((6, ns, GROUP, CELLS), BF16),
            pltpu.VMEM((6, ns, GROUP, CELLS), BF16),
            pltpu.VMEM((3, GROUP, 16, width), BF16),
            pltpu.VMEM((3, GROUP, 16, width), BF16),
            pltpu.VMEM((3, nd, 16, width), BF16),
            pltpu.VMEM((3, nd, 16, width), BF16),
            pltpu.SemaphoreType.DMA((12,)),
            pltpu.SemaphoreType.DMA((12,)),
        ],
        compiler_params=pltpu.CompilerParams(
            collective_id=0, has_side_effects=True, vmem_limit_bytes=48 * 1024 * 1024
        ),
    )(pair_rep, cotangent, residue_mask[None, :], w_proj, w_gate, w_out)


def solution(mesh):
    nd, ns = mesh.shape["dap"], mesh.shape["ch"]
    return jax.shard_map(
        functools.partial(on_device, nd, ns),
        mesh=mesh,
        in_specs=(P("dap", "ch", None), P(), P(), P(), P(), P("dap", "ch", None)),
        out_specs=(P("dap", "ch", None), P("dap", "ch", None)),
        check_vma=False,
    )
```

time: 228 us -> 85.6 us (0.38)
  the two profiles are of different devices: /device:TPU:1 before, /device:TPU:18 now
where the time goes in v1:
time: 85.6 us; the launch traced here: 85.2 us
  Pallas kernels  78.4 us (92%)
  local copies, waits for them, and re-layouts  6.19 us (7%)
    pallas_call x1, Pallas kernels, on_device(): pl.pallas_call(functools.partial(kernel, nd, ns), out_shape=(shape, shape...  78.4 us
    unnamed x14, local copies, waits for them, and re-layouts  6.19 us

profile of v1, /device:TPU:18, one launch (start us, length us, event | category | flops | bytes accessed | tf_op | source)
XLA Modules:
  0.0 85.2 jit_solution(10558682816287272066)
XLA Ops:
  0.6 0.0 copy-start
  0.6 0.9 %copy-done = bf16[128,512]{1,0:T(8,128)(2,1)S(1)} copy-done((bf16[128,512]{1,0:T(8,128)(2,1)S(1)}, bf16[128,512]{1,0:T(8,128)(2,1)}, u32[]{:S(2)}) %copy-start) | copy-done | bytes 131096
  1.5 0.0 copy-start.1
  1.5 0.9 %copy-done.1 = bf16[15,30,128]{2,1,0:T(8,128)(2,1)S(1)} copy-done((bf16[15,30,128]{2,1,0:T(8,128)(2,1)S(1)}, bf16[15,30,128]{2,1,0:T(8,128)(2,1)}, u32[]{:S(2)}) %copy-start.1) | copy-done | bytes 115224
  2.4 0.0 copy-start.2
  2.4 0.9 %copy-done.2 = bf16[15,30,128]{2,1,0:T(8,128)(2,1)S(1)} copy-done((bf16[15,30,128]{2,1,0:T(8,128)(2,1)S(1)}, bf16[15,30,128]{2,1,0:T(8,128)(2,1)}, u32[]{:S(2)}) %copy-start.2) | copy-done | bytes 115224
  3.3 0.0 copy-start.3
  3.3 0.8 copy-done.3
  4.1 0.0 copy-start.4
  4.1 0.8 copy-done.4
  4.9 0.0 copy-start.5
  4.9 0.7 copy-done.5
  5.5 78.4 %shard_map.77 = (bf16[15,30,128]{2,1,0:T(8,128)(2,1)S(1)}, bf16[15,30,128]{2,1,0:T(8,128)(2,1)S(1)}) custom-call(bf16[15,30,128]{2,1,0:T(8,128)(2,1)S(1)} %copy-done.1, bf16[15,30,128]{2,1,0:T(8,128)(2,1)S(1)} %copy-done.2, s32[1,480]{1,0:T(1,128)S(1)} %bitcast.1, bf16[128,512]{1,0:T(8,128)(2,1)S(1)} %copy-done, bf16[128,128]{1,0:T(8,128)(2,1)S(1)} %copy-done.3, ...), custom_call_target="tpu_custom_call" | custom-call | tf_op jit(solution)/shard_map/pallas_call | solution.py:389
  83.9 0.7 copy.10
  84.6 0.6 copy.11
Async XLA Ops:
  0.6 0.9 %copy-start = (bf16[128,512]{1,0:T(8,128)(2,1)S(1)}, bf16[128,512]{1,0:T(8,128)(2,1)}, u32[]{:S(2)}) copy-start(bf16[128,512]{1,0:T(8,128)(2,1)} %wp_ref.1) | copy-start | bytes 393220
  1.5 0.9 %copy-start.1 = (bf16[15,30,128]{2,1,0:T(8,128)(2,1)S(1)}, bf16[15,30,128]{2,1,0:T(8,128)(2,1)}, u32[]{:S(2)}) copy-start(bf16[15,30,128]{2,1,0:T(8,128)(2,1)} %x_ref.1) | copy-start | bytes 345604
  2.4 0.9 %copy-start.2 = (bf16[15,30,128]{2,1,0:T(8,128)(2,1)S(1)}, bf16[15,30,128]{2,1,0:T(8,128)(2,1)}, u32[]{:S(2)}) copy-start(bf16[15,30,128]{2,1,0:T(8,128)(2,1)} %cot_ref.1) | copy-start | bytes 345604
  3.3 0.8 copy-start.3
  4.1 0.8 copy-start.4
  4.9 0.7 copy-start.5

commit v2 on v1

--- a/solution.py
+++ b/solution.py
@@ -25,6 +25,31 @@
         z = lax.rem(me // 2, 8)
         return z, jnp.logical_and(lax.rem(me, 2) == 1, me // 16 == lax.rem(z, 2))
     return me, me < GROUP
+
+
+def ring_order(size):
+    return sorted(range(size), key=lambda r: -min(r, size - r))
+
+
+def ch_peers(me, ch_size):
+    ny = ch_size // 2
+    steps = [(dy, dx) for dy in range(ny) for dx in range(2) if dy or dx]
+    steps.sort(key=lambda p: -(min(p[0], ny - p[0]) + 2 * p[1]))
+    y, x = me // 2, lax.rem(me, 2)
+    return [2 * lax.rem(y + dy, ny) + lax.rem(x + dx, 2) for dy, dx in steps]
+
+
+def dap_peers(me, dap_size):
+    if dap_size != 32:
+        return [lax.rem(me + r, dap_size) for r in range(1, dap_size)]
+    x, z = me // 16, lax.rem(me // 2, 8)
+    return [
+        16 * lax.rem(x + dx, 2) + 2 * lax.rem(z + dz, 8) + core
+        for dz in ring_order(8)
+        for dx in (1, 0)
+        for core in (0, 1)
+        if dz or dx or not core
+    ]
 
 
 def dot(a, b, contract):
@@ -75,14 +100,20 @@
 def kernel(
     nd,
     ns,
+    x_hbm,
+    cot_hbm,
+    mask_hbm,
+    wp_hbm,
+    wg_hbm,
+    wo_hbm,
+    upd_ref,
+    gpair_ref,
     x_ref,
     cot_ref,
     mask_ref,
     wp_ref,
     wg_ref,
     wo_ref,
-    upd_ref,
-    gpair_ref,
     padded,
     live,
     proj,
@@ -98,6 +129,7 @@
     in2,
     own_in,
     own_out,
+    load_sem,
     send_sem,
     recv_sem,
 ):
@@ -108,6 +140,22 @@
     me_s = lax.axis_index("ch")
     my_m, is_owner = owned_by(me_d, nd)
 
+    loads = [
+        pltpu.make_async_copy(src, dst, load_sem.at[n])
+        for n, (src, dst) in enumerate(
+            (
+                (x_hbm, x_ref),
+                (wp_hbm, wp_ref),
+                (mask_hbm, mask_ref),
+                (cot_hbm, cot_ref),
+                (wg_hbm, wg_ref),
+                (wo_hbm, wo_ref),
+            )
+        )
+    ]
+    for load in loads:
+        load.start()
+
     barrier = pltpu.get_barrier_semaphore()
 
     def greet(peer):
@@ -115,21 +163,18 @@
             barrier, inc=1, device_id=peer, device_id_type=pl.DeviceIdType.MESH
         )
 
-    @pl.loop(1, ns)
-    def _(r):
-        greet({"ch": lax.rem(me_s + r, ns)})
+    for peer in ch_peers(me_s, ns):
+        greet({"ch": peer})
 
     @pl.when(is_owner)
     def _():
-        @pl.loop(1, nd)
-        def _(r):
-            greet({"dap": lax.rem(me_d + r, nd)})
+        for peer in dap_peers(me_d, nd):
+            greet({"dap": peer})
 
     @pl.when(jnp.logical_not(is_owner))
     def _():
-        @pl.loop(0, GROUP)
-        def _(m):
-            greet({"dap": owner_of(m, nd)})
+        for r in ring_order(GROUP):
+            greet({"dap": owner_of(lax.rem(my_m + r, GROUP), nd)})
 
     def push(src, dst, sem, peer):
         return pltpu.make_async_remote_copy(
@@ -142,11 +187,8 @@
         )
 
     def across_ch(src, dst, sem):
-        @pl.loop(1, ns)
-        def _(r):
-            peer = lax.rem(me_s + r, ns)
+        for peer in ch_peers(me_s, ns):
             push(src.at[peer], dst.at[me_s], sem, {"ch": peer}).start()
-
         dst[me_s] = src[me_s]
 
     def await_ch(dst, sem):
@@ -154,31 +196,23 @@
         push(some, some, sem, {"ch": me_s}).wait_recv()
 
     def to_owners(src, dst, sem):
-        @pl.loop(0, GROUP)
-        def _(r):
-            m = lax.rem(my_m + r, GROUP)
-            owner = owner_of(m, nd)
-
-            @pl.when(owner != me_d)
-            def _():
-                push(src.at[m], dst.at[me_d], sem, {"dap": owner}).start()
-
-            @pl.when(owner == me_d)
-            def _():
-                dst[me_d] = src[m]
+        def send(m):
+            push(src.at[m], dst.at[me_d], sem, {"dap": owner_of(m, nd)}).start()
+
+        for r in ring_order(GROUP)[:-1]:
+            send(lax.rem(my_m + r, GROUP))
+
+        @pl.when(is_owner)
+        def _():
+            dst[me_d] = src[my_m]
+
+        @pl.when(jnp.logical_not(is_owner))
+        def _():
+            send(my_m)
 
     def await_owner(dst, sem):
         some = dst.at[pl.ds(0, nd - 1)]
         push(some, some, sem, {"dap": me_d}).wait_recv()
-
-    def from_owner(src, dst, sem, d):
-        @pl.when(d != me_d)
-        def _():
-            push(src.at[d], dst.at[my_m], sem, {"dap": d}).start()
-
-        @pl.when(d == me_d)
-        def _():
-            dst[my_m] = src[d]
 
     def await_rows(dst, sem):
         @pl.when(is_owner)
@@ -214,6 +248,7 @@
         )
         return closed.T.reshape(16, 32, chans)[0:rows, 0:columns, :].astype(BF16)
 
+    loads[0].wait()
     xt = cells_first(x_ref, 0)
     center = jnp.mean(xt, axis=0, keepdims=True)
     spread = xt - center
@@ -224,6 +259,7 @@
 
     residues = mask_ref.shape[1]
     total = nd * 16
+    loads[2].wait()
     live[...] = jnp.zeros(live.shape, F32)
     live[:, 0:residues] = jnp.broadcast_to(mask_ref[...].astype(F32), (8, residues))
     flags = live[...].astype(BF16)
@@ -257,12 +293,15 @@
         proj[part + 1] = val
         out1[slot] = (sig * val * mask).reshape(ns, GROUP, CELLS).astype(BF16)
 
+    loads[1].wait()
     edge(0, 0)
     pl.semaphore_wait(barrier, ns - 1 + jnp.where(is_owner, nd - 1, GROUP))
     across_ch(out1.at[0], in1.at[0], 0)
     edge(2, 1)
     across_ch(out1.at[1], in1.at[1], 1)
 
+    for load in loads[3:]:
+        load.wait()
     gv = jax.nn.sigmoid(dot(wg_ref[...], nh, ((0,), (0,))))
     gate[...] = gv
     ct = cells_first(cot_ref, 1)
@@ -276,27 +315,26 @@
         to_owners(out2.at[a], own_in.at[a], 2 + a)
 
     width = ns * 32
-    per = 128 // 16
-
-    def all_rows(ref):
-        return ref[...].reshape(nd * 16, width)
-
-    def return_rows(buffer, back, sem, b, value):
-        own_out[buffer, pl.ds(per * b, per)] = value.astype(BF16).reshape(per, 16, width)
-
-        @pl.loop(0, per)
-        def _(e):
-            from_owner(own_out.at[buffer], in2.at[back], sem, per * b + e)
+    many = nd * 16
+
+    def multiply(a, b, contract, buffer, back, sem):
+        right = own_in[b].reshape(many, width)
+        for h in range(2):
+            if contract[0][0] == 1:
+                part = own_in[a, pl.ds(h * nd // 2, nd // 2)].reshape(many // 2, width)
+            else:
+                part = own_in[a, :, :, pl.ds(h * width // 2, width // 2)].reshape(many, width // 2)
+            value = dot(part, right, contract).astype(BF16)
+            own_out[buffer, pl.ds(h * nd // 2, nd // 2)] = value.reshape(nd // 2, 16, width)
+        for d in dap_peers(me_d, nd):
+            push(own_out.at[buffer, d], in2.at[back, my_m], sem, {"dap": d}).start()
+        in2[back, my_m] = own_out[buffer, me_d]
 
     @pl.when(is_owner)
     def _():
         await_owner(own_in.at[0], 2)
         await_owner(own_in.at[1], 3)
-
-        @pl.loop(0, nd // per)
-        def _(b):
-            left = own_in[0, pl.ds(per * b, per)].reshape(128, width)
-            return_rows(0, 0, 4, b, dot(left, all_rows(own_in.at[1]), ((1,), (1,))))
+        multiply(0, 1, ((1,), (1,)), 0, 0, 4)
 
     await_rows(in2.at[0], 4)
     rows_to_cells(in2.at[0], mid, out1.at[2])
@@ -325,17 +363,8 @@
     @pl.when(is_owner)
     def _():
         await_owner(own_in.at[2], 7)
-
-        @pl.loop(0, nd // per)
-        def _(b):
-            part = own_in[2, pl.ds(per * b, per)].reshape(128, width)
-            return_rows(1, 1, 8, b, dot(part, all_rows(own_in.at[1]), ((1,), (0,))))
-
-        @pl.loop(0, nd // per)
-        def _(b):
-            lanes = pl.ds(pl.multiple_of(b * 128, 128), 128)
-            part = own_in[2, :, :, lanes].reshape(nd * 16, 128)
-            return_rows(2, 2, 9, b, dot(part, all_rows(own_in.at[0]), ((0,), (0,))))
+        multiply(2, 1, ((1,), (0,)), 1, 1, 8)
+        multiply(2, 0, ((0,), (0,)), 2, 2, 9)
 
     base = dot(wg_ref[...], glogit[...], ((1,), (0,)))
 
@@ -381,17 +410,32 @@
             sent(own_out.at[buffer, pl.ds(0, nd - 1)], sem)
 
 
+def to_hbm(upd, gpair, upd_hbm, gpair_hbm, sem):
+    copies = [
+        pltpu.make_async_copy(upd, upd_hbm, sem.at[0]),
+        pltpu.make_async_copy(gpair, gpair_hbm, sem.at[1]),
+    ]
+    for copy in copies:
+        copy.start()
+    for copy in copies:
+        copy.wait()
+
+
 def on_device(nd, ns, pair_rep, residue_mask, w_proj, w_gate, w_out, cotangent):
     hidden, chans = w_out.shape
     vmem = pl.BlockSpec(memory_space=pltpu.VMEM)
+    hbm = pl.BlockSpec(memory_space=pltpu.HBM)
     shape = jax.ShapeDtypeStruct(pair_rep.shape, BF16)
     width = ns * 32
-    return pl.pallas_call(
+    args = (pair_rep, cotangent, residue_mask[None, :], w_proj, w_gate, w_out)
+    args = [pltpu.with_memory_space_constraint(a, pltpu.HBM) for a in args]
+    results = pl.pallas_call(
         functools.partial(kernel, nd, ns),
         out_shape=(shape, shape),
-        in_specs=[vmem] * 6,
+        in_specs=[hbm] * 6,
         out_specs=(vmem, vmem),
-        scratch_shapes=[
+        scratch_shapes=[pltpu.VMEM(a.shape, a.dtype) for a in args]
+        + [
             pltpu.VMEM((2, 16, 32, chans), BF16),
             pltpu.VMEM((8, nd * 16), F32),
             pltpu.VMEM((4, hidden, CELLS), F32),
@@ -407,13 +451,22 @@
             pltpu.VMEM((3, GROUP, 16, width), BF16),
             pltpu.VMEM((3, nd, 16, width), BF16),
             pltpu.VMEM((3, nd, 16, width), BF16),
+            pltpu.SemaphoreType.DMA((6,)),
             pltpu.SemaphoreType.DMA((12,)),
             pltpu.SemaphoreType.DMA((12,)),
         ],
         compiler_params=pltpu.CompilerParams(
-            collective_id=0, has_side_effects=True, vmem_limit_bytes=48 * 1024 * 1024
+            collective_id=0, has_side_effects=True, vmem_limit_bytes=50331648
         ),
-    )(pair_rep, cotangent, residue_mask[None, :], w_proj, w_gate, w_out)
+    )(*args)
+    return pl.pallas_call(
+        to_hbm,
+        out_shape=(shape, shape),
+        in_specs=[vmem, vmem],
+        out_specs=(hbm, hbm),
+        scratch_shapes=[pltpu.SemaphoreType.DMA((2,))],
+        compiler_params=pltpu.CompilerParams(vmem_limit_bytes=1024 * 1024),
+    )(*results)
 
 
 def solution(mesh):

time: 85.6 us -> 75 us (0.88)
  the two profiles are of different devices: /device:TPU:18 before, /device:TPU:1 now
where the time goes in v2:
time: 75 us; the launch traced here: 74.9 us
  Pallas kernels  74.2 us (99%)
    pallas_call x1, Pallas kernels, on_device(): pl.pallas_call(functools.partial(kernel, nd, ns), out_shape=(shape, shape...  73.5 us

profile of v2, /device:TPU:1, one launch (start us, length us, event | category | flops | bytes accessed | tf_op | source)
XLA Modules:
  0.0 74.9 jit_solution(14526197690726085469)
XLA Ops:
  0.6 73.5 %shard_map.77 = (bf16[15,30,128]{2,1,0:T(8,128)(2,1)S(1)}, bf16[15,30,128]{2,1,0:T(8,128)(2,1)S(1)}) custom-call(bf16[15,30,128]{2,1,0:T(8,128)(2,1)} %x_hbm.1, bf16[15,30,128]{2,1,0:T(8,128)(2,1)} %cot_hbm.1, s32[1,480]{1,0:T(1,128)} %bitcast.1, bf16[128,512]{1,0:T(8,128)(2,1)} %wp_hbm.1, bf16[128,128]{1,0:T(8,128)(2,1)} %wg_hbm.1, bf16[128,128]{1,0:T(8,128)(2,1)} %wo_hbm.1), custom_call_target="tpu_custom_call" | custom-call | tf_op jit(solution)/shard_map/pallas_call | solution.py:432
  74.2 0.7 shard_map.78

commit v3 on v2

v3 whole, which is shorter than its diff:
```python
import functools

import jax
import jax.numpy as jnp
from jax import lax
from jax.experimental import pallas as pl
from jax.experimental.pallas import tpu as pltpu
from jax.sharding import PartitionSpec as P

EPSILON = 1e-05
F32 = jnp.float32
BF16 = jnp.bfloat16
CELLS = 512
QUADS = CELLS // 128


def ring_order(size):
    return sorted(range(size), key=lambda r: -min(r, size - r))


def ch_peers(me, ch_size):
    ny = ch_size // 2
    steps = [(dy, dx) for dy in range(ny) for dx in range(2) if dy or dx]
    steps.sort(key=lambda p: -(min(p[0], ny - p[0]) + 2 * p[1]))
    y, x = me // 2, lax.rem(me, 2)
    return [2 * lax.rem(y + dy, ny) + lax.rem(x + dx, 2) for dy, dx in steps]


def dot(a, b, contract):
    return lax.dot_general(a, b, (contract, ((), ())), preferred_element_type=F32)


def swap_blocks(rows):
    block = lax.broadcasted_iota(jnp.int32, rows[0].shape, 1) // 32
    odd = lax.rem(block, 2) == 1
    high = block >= 2
    x0, x1, x2, x3 = rows
    z0 = jnp.where(odd, pltpu.roll(x1, 32, 1), x0)
    z1 = jnp.where(odd, x1, pltpu.roll(x0, 96, 1))
    z2 = jnp.where(odd, pltpu.roll(x3, 32, 1), x2)
    z3 = jnp.where(odd, x3, pltpu.roll(x2, 96, 1))
    return (
        jnp.where(high, pltpu.roll(z2, 64, 1), z0),
        jnp.where(high, pltpu.roll(z3, 64, 1), z1),
        jnp.where(high, z2, pltpu.roll(z0, 64, 1)),
        jnp.where(high, z3, pltpu.roll(z1, 64, 1)),
    )


def cells_to_rows(cells, first, count, mid, rows, place):
    group = cells.shape[1]
    for t in range(count // 4):
        for q in range(QUADS):
            lanes = pl.ds(q * 128, 128)
            moved = swap_blocks([cells[first + 4 * t + a, :, lanes].astype(F32) for a in range(4)])
            for b in range(4):
                mid[t, pl.ds(4 * q + b, group, stride=16), :] = moved[b]
    for t in range(count // 4):
        for m in range(group):
            rows[place(m), :, pl.ds(t * 128, 128)] = mid[t, pl.ds(16 * m, 16), :].astype(BF16)


def rows_to_cells(rows, place, mid, cells, first, count):
    group = cells.shape[1]
    for t in range(count // 4):
        for m in range(group):
            mid[t, pl.ds(16 * m, 16), :] = rows[place(m), :, pl.ds(t * 128, 128)].astype(F32)
    for t in range(count // 4):
        for q in range(QUADS):
            lanes = pl.ds(q * 128, 128)
            moved = swap_blocks([mid[t, pl.ds(4 * q + b, group, stride=16), :] for b in range(4)])
            for a in range(4):
                cells[first + 4 * t + a, :, lanes] = moved[a].astype(BF16)


def swap_leading(src, mid, dst):
    na, nb = src.shape[0], src.shape[1]
    for q in range(QUADS):
        lanes = pl.ds(q * 128, 128)
        for a in range(na):
            mid[q, pl.ds(a * nb, nb), :] = src[a, :, lanes].astype(F32)
        for b in range(nb):
            dst[b, :, lanes] = mid[q, pl.ds(b, na, stride=nb), :].astype(BF16)


def kernel(
    nd,
    ns,
    x_hbm,
    cot_hbm,
    mask_hbm,
    wp_hbm,
    wg_hbm,
    wo_hbm,
    upd_ref,
    gpair_ref,
    x_ref,
    cot_ref,
    mask_ref,
    wp_ref,
    wg_ref,
    wo_ref,
    padded,
    live,
    proj,
    normed,
    gate,
    cot,
    ghid,
    glogit,
    mid,
    ch_out,
    ch_in,
    row_out,
    row_in,
    own_in,
    own_out,
    z_out,
    z_in,
    col_out,
    col_in,
    own_cells_in,
    own_cells_out,
    load_sem,
    send_sem,
    recv_sem,
):
    rows, columns, chans = x_ref.shape
    half = columns // 2
    nz = nd // 4
    hidden = ns * nz
    me_d = lax.axis_index("dap")
    me_s = lax.axis_index("ch")
    my_x, my_z, my_core = me_d // (2 * nz), lax.rem(me_d // 2, nz), lax.rem(me_d, 2)
    is_owner = jnp.logical_and(my_core == 1, my_x == lax.rem(my_z + me_s // 2, 2))

    def at_dap(x, z, core):
        return 2 * nz * x + 2 * z + core

    def owner_of(z, s):
        return at_dap(lax.rem(z + s // 2, 2), z, 1)

    near_ch = ch_peers(me_s, ns)
    z_order = [lax.rem(my_z + r, nz) for r in ring_order(nz)]
    other_x = 1 - my_x
    dap_order = [
        at_dap(x, z, core)
        for z in z_order
        for x in (other_x, my_x)
        for core in (0, 1)
    ][:-1]
    quarters = [(other_x, 0), (other_x, 1), (my_x, 0), (my_x, 1)]

    loads = [
        pltpu.make_async_copy(src, dst, load_sem.at[n])
        for n, (src, dst) in enumerate(
            (
                (x_hbm, x_ref),
                (wp_hbm, wp_ref),
                (mask_hbm, mask_ref),
                (cot_hbm, cot_ref),
                (wg_hbm, wg_ref),
                (wo_hbm, wo_ref),
            )
        )
    ]
    for load in loads:
        load.start()

    barrier = pltpu.get_barrier_semaphore()

    def greet(peer):
        pl.semaphore_signal(
            barrier, inc=1, device_id=peer, device_id_type=pl.DeviceIdType.MESH
        )

    for s in near_ch:
        greet({"ch": s})
    for z in z_order[:-1]:
        greet({"dap": at_dap(my_x, z, my_core)})

    @pl.when(is_owner)
    def _():
        for d in dap_order:
            greet({"dap": d})
        for x, core in quarters:
            for s in near_ch:
                greet({"dap": at_dap(x, my_z, core), "ch": s})
        for x, core in quarters[:-1]:
            greet({"dap": at_dap(x, my_z, core), "ch": me_s})

    @pl.when(jnp.logical_not(is_owner))
    def _():
        for z in z_order:
            greet({"dap": owner_of(z, me_s)})
        for s in near_ch + [me_s]:
            greet({"dap": owner_of(my_z, s), "ch": s})

    greetings = (
        ns - 1 + nz - 1 + jnp.where(is_owner, nd - 1 + 4 * ns - 1, nz + ns)
    )

    def push(src, dst, sem, peer, arrival=None):
        return pltpu.make_async_remote_copy(
            src_ref=src,
            dst_ref=dst,
            send_sem=send_sem.at[sem],
            recv_sem=recv_sem.at[sem if arrival is None else arrival],
            device_id=peer,
            device_id_type=pl.DeviceIdType.MESH,
        )

    def await_slabs(ref, count, sem):
        some = ref.at[pl.ds(0, count)]
        push(some, some, sem, {"dap": me_d}).wait_recv()

    def await_all_but_mine(ref, sem):
        @pl.when(is_owner)
        def _():
            await_slabs(ref, ref.shape[0] - 1, sem)

        @pl.when(jnp.logical_not(is_owner))
        def _():
            await_slabs(ref, ref.shape[0], sem)

    def across_ch(n, sem):
        src, dst = ch_out.at[n], ch_in.at[n]
        for s in near_ch:
            push(src.at[s], dst.at[me_s], sem, {"ch": s}).start()
        dst[me_s] = src[me_s]

    def await_ch(n, sem):
        await_slabs(ch_in.at[n], ns - 1, sem)

    def across_z(n, sem):
        src, dst = z_out.at[n], z_in.at[n]
        for z in z_order[:-1]:
            push(src.at[z], dst.at[my_z], sem, {"dap": at_dap(my_x, z, my_core)}).start()
        dst[my_z] = src[my_z]

    def await_z(n, sem):
        await_slabs(z_in.at[n], nz - 1, sem)

    def rows_to_owners(n, a, sem):
        src, dst = row_out.at[n], own_in.at[a]

        def send(z):
            push(src.at[z], dst.at[me_d], sem, {"dap": owner_of(z, me_s)}).start()

        for z in z_order[:-1]:
            send(z)

        @pl.when(is_owner)
        def _():
            dst[me_d] = src[my_z]

        @pl.when(jnp.logical_not(is_owner))
        def _():
            send(my_z)

    def columns_to_owners(sem):
        quarter = 2 * my_x + my_core
        slot = quarter * ns + me_s

        def send(s):
            peer = {"dap": owner_of(my_z, s), "ch": s}
            push(col_out.at[s], own_cells_in.at[slot], sem, peer, 12 + quarter).start()

        for s in near_ch:
            send(s)

        @pl.when(is_owner)
        def _():
            own_cells_in[slot] = col_out[me_s]

        @pl.when(jnp.logical_not(is_owner))
        def _():
            send(me_s)

    lane = lax.broadcasted_iota(jnp.int32, (1, CELLS), 1)
    place = lax.rem(lane, 16)
    used = jnp.logical_and(place < half, lane < rows * 32)
    first_half = lax.rem(lane, 32) < 16

    eye = (
        lax.broadcasted_iota(jnp.int32, (chans, chans), 0)
        == lax.broadcasted_iota(jnp.int32, (chans, chans), 1)
    ).astype(F32).astype(BF16)

    def cells_first(ref, slot):
        padded[slot] = jnp.zeros(padded.shape[1:], BF16)
        padded[slot, 0:rows, 0:columns, :] = ref[...]
        flat = padded[slot].reshape(CELLS, chans)
        turned = dot(eye, flat, ((1,), (1,)))
        spread = jnp.where(first_half, turned, pltpu.roll(turned, 1, 1))
        return jnp.where(used, spread, 0.0)

    def cells_last(turned):
        closed = jnp.where(
            lax.rem(lane, 32) < half, turned, pltpu.roll(turned, CELLS - 1, 1)
        )
        return closed.T.reshape(16, 32, chans)[0:rows, 0:columns, :].astype(BF16)

    loads[0].wait()
    xt = cells_first(x_ref, 0)
    center = jnp.mean(xt, axis=0, keepdims=True)
    spread = xt - center
    pair_scale = lax.rsqrt(jnp.mean(spread * spread, axis=0, keepdims=True) + EPSILON)
    nt = spread * pair_scale
    normed[...] = nt
    nh = nt.astype(BF16)

    residues = mask_ref.shape[1]
    total = nd * 16
    loads[2].wait()
    live[...] = jnp.zeros(live.shape, F32)
    live[:, 0:residues] = jnp.broadcast_to(mask_ref[...].astype(F32), (8, residues))
    flags = live[...].astype(BF16)

    def one_hot(hot):
        return jnp.where(hot, 1.0, 0.0).astype(BF16)

    at = lax.broadcasted_iota(jnp.int32, (total, 128), 0)
    lane_1 = lax.broadcasted_iota(jnp.int32, (total, 128), 1)
    row_flags = dot(
        flags, one_hot(jnp.logical_and(at == rows * me_d + lane_1, lane_1 < rows)), ((1,), (0,))
    )
    col_at = columns * me_s + half * (lax.rem(lane_1, 32) // 16) + lax.rem(lane_1, 16)
    col_flags = dot(
        flags, one_hot(jnp.logical_and(at == col_at, lax.rem(lane_1, 16) < half)), ((1,), (0,))
    )
    spot = lax.broadcasted_iota(jnp.int32, (128, CELLS), 0)
    row_of = lax.broadcasted_iota(jnp.int32, (128, CELLS), 1) // 32
    row_mask = dot(row_flags.astype(BF16), one_hot(spot == row_of), ((1,), (0,)))
    col_mask = jnp.concatenate([col_flags] * (CELLS // 128), axis=1)
    mask = (row_mask * col_mask)[0:1]

    def project(part):
        raw = dot(wp_ref[:, pl.ds(part * hidden, hidden)], nh, ((0,), (0,)))
        return raw

    def edge(part):
        sig = jax.nn.sigmoid(project(part))
        val = project(part + 1)
        proj[part] = sig
        proj[part + 1] = val
        return sig * val * mask

    loads[1].wait()
    ch_out[0] = edge(0).reshape(ns, nz, CELLS).astype(BF16)
    right = edge(2)
    for q in range(QUADS):
        lanes = slice(q * 128, q * 128 + 128)
        mid[q, 0:hidden, :] = right[:, lanes]
        for z in range(nz):
            z_out[0, z, :, lanes] = mid[q, pl.ds(z, ns, stride=nz), :].astype(BF16)
    pl.semaphore_wait(barrier, greetings)
    across_z(0, 1)
    across_ch(0, 0)

    for load in loads[3:]:
        load.wait()
    gv = jax.nn.sigmoid(dot(wg_ref[...], nh, ((0,), (0,))))
    gate[...] = gv
    ct = cells_first(cot_ref, 1)
    cot[...] = ct
    gh = dot(wo_ref[...], (ct * gv).astype(BF16), ((1,), (0,)))
    ghid[...] = gh - jnp.mean(gh, axis=0, keepdims=True)

    await_z(0, 1)
    swap_leading(z_in.at[0], mid, col_out)
    columns_to_owners(3)
    await_ch(0, 0)
    cells_to_rows(ch_in.at[0], 0, ns, mid, row_out.at[0], lambda m: m)
    rows_to_owners(0, 0, 2)

    width = ns * 32
    many = nd * 16

    def multiply(a, b, contract, n):
        right = own_in[b].reshape(many, width)
        for h in range(2):
            if contract[0][0] == 1:
                part = own_in[a, pl.ds(h * nd // 2, nd // 2)].reshape(many // 2, width)
            else:
                part = own_in[a, :, :, pl.ds(h * width // 2, width // 2)].reshape(many, width // 2)
            value = dot(part, right, contract).astype(BF16)
            own_out[n, pl.ds(h * nd // 2, nd // 2)] = value.reshape(nd // 2, 16, width)

    def rows_back(n, sem):
        src, dst = own_out.at[n], row_in.at[n]
        for d in dap_order:
            push(src.at[d], dst.at[my_z], sem, {"dap": d}).start()
        dst[my_z] = src[me_d]

    def columns_back(n, sem):
        for g, (x, core) in enumerate(quarters):
            rows_to_cells(
                own_out.at[n],
                lambda z, x=x, core=core: at_dap(x, z, core),
                mid,
                own_cells_out,
                g * ns,
                ns,
            )
            d = at_dap(x, my_z, core)
            for s in near_ch + ([me_s] if g < 3 else []):
                push(
                    own_cells_out.at[g * ns + s], col_in.at[me_s], sem, {"dap": d, "ch": s}
                ).start()
        col_in[me_s] = own_cells_out[3 * ns + me_s]

    @pl.when(is_owner)
    def _():
        def arrived(x, core, count):
            quarter = 2 * x + core
            await_slabs(own_cells_in, count, 12 + quarter)
            cells_to_rows(
                own_cells_in,
                quarter * ns,
                ns,
                mid,
                own_in.at[1],
                lambda z: at_dap(x, z, core),
            )

        arrived(my_x, 1, ns - 1)

        @pl.loop(0, 3)
        def _(r):
            arrived(jnp.where(r == 0, my_x, other_x), lax.rem(r, 2), ns)

        await_slabs(own_in.at[0], nd - 1, 2)
        multiply(0, 1, ((1,), (1,)), 0)
        rows_back(0, 4)

    await_all_but_mine(row_in.at[0], 4)
    rows_to_cells(row_in.at[0], lambda m: m, mid, ch_out.at[1], 0, ns)
    across_ch(1, 5)
    await_ch(1, 5)

    prod = ch_in[1].reshape(hidden, CELLS).astype(F32)
    away = prod - jnp.mean(prod, axis=0, keepdims=True)
    hidden_scale = lax.rsqrt(jnp.mean(away * away, axis=0, keepdims=True) + EPSILON)
    hn = away * hidden_scale
    gh_away = ghid[...]
    second = jnp.mean((gh_away) * hn, axis=0, keepdims=True)
    gprod = hidden_scale * (gh_away - hn * second)
    ch_out[2] = gprod.reshape(ns, nz, CELLS).astype(BF16)
    across_ch(2, 6)

    po = dot(wo_ref[...], hn.astype(BF16), ((0,), (0,)))
    gv = gate[...]
    glogit[...] = (cot[...] * po * gv * (1.0 - gv)).astype(BF16)
    upd_ref[...] = cells_last(gv * po)

    await_ch(2, 6)
    cells_to_rows(ch_in.at[2], 0, ns, mid, row_out.at[1], lambda m: m)
    rows_to_owners(1, 2, 7)

    @pl.when(is_owner)
    def _():
        await_slabs(own_in.at[2], nd - 1, 7)
        multiply(2, 1, ((1,), (0,)), 1)
        rows_back(1, 8)
        multiply(2, 0, ((0,), (0,)), 2)
        columns_back(2, 9)

    base = dot(wg_ref[...], glogit[...], ((1,), (0,)))

    def through(base, part, back):
        masked = back * mask
        sig = proj[part]
        val = proj[part + 1]
        to_sig = (masked * val * sig * (1.0 - sig)).astype(BF16)
        to_val = (masked * sig).astype(BF16)
        base = base + dot(wp_ref[:, pl.ds(part * hidden, hidden)], to_sig, ((1,), (0,)))
        return base + dot(wp_ref[:, pl.ds((part + 1) * hidden, hidden)], to_val, ((1,), (0,)))

    await_all_but_mine(row_in.at[1], 8)
    rows_to_cells(row_in.at[1], lambda m: m, mid, ch_out.at[3], 0, ns)
    across_ch(3, 10)
    await_all_but_mine(col_in, 9)
    swap_leading(col_in, mid, z_out.at[1])
    across_z(1, 11)
    await_ch(3, 10)
    base = through(base, 0, ch_in[3].reshape(hidden, CELLS).astype(F32))
    await_z(1, 11)
    for q in range(QUADS):
        lanes = slice(q * 128, q * 128 + 128)
        for z in range(nz):
            mid[q, pl.ds(z, ns, stride=nz), :] = z_in[1, z, :, lanes].astype(F32)
    back = jnp.concatenate([mid[q, 0:hidden, :] for q in range(QUADS)], axis=1)
    base = through(base, 2, back)

    nt = normed[...]
    first = jnp.mean(base, axis=0, keepdims=True)
    second = jnp.mean(base * nt, axis=0, keepdims=True)
    gpair_ref[...] = cells_last(pair_scale * (base - first - nt * second))

    def sent(ref, count, sem):
        some = ref.at[pl.ds(0, count)]
        push(some, some, sem, {"dap": me_d}).wait_send()

    for n, sem in ((0, 0), (1, 5), (2, 6), (3, 10)):
        sent(ch_out.at[n], ns - 1, sem)
    for n, sem in ((0, 1), (1, 11)):
        sent(z_out.at[n], nz - 1, sem)

    @pl.when(is_owner)
    def _():
        sent(row_out.at[0], nz - 1, 2)
        sent(row_out.at[1], nz - 1, 7)
        sent(col_out, ns - 1, 3)
        sent(own_out.at[0], nd - 1, 4)
        sent(own_out.at[1], nd - 1, 8)
        sent(own_cells_out, 4 * ns - 1, 9)

    @pl.when(jnp.logical_not(is_owner))
    def _():
        sent(row_out.at[0], nz, 2)
        sent(row_out.at[1], nz, 7)
        sent(col_out, ns, 3)


def to_hbm(upd, gpair, upd_hbm, gpair_hbm, sem):
    copies = [
        pltpu.make_async_copy(upd, upd_hbm, sem.at[0]),
        pltpu.make_async_copy(gpair, gpair_hbm, sem.at[1]),
    ]
    for copy in copies:
        copy.start()
    for copy in copies:
        copy.wait()


def on_device(nd, ns, pair_rep, residue_mask, w_proj, w_gate, w_out, cotangent):
    hidden, chans = w_out.shape
    vmem = pl.BlockSpec(memory_space=pltpu.VMEM)
    hbm = pl.BlockSpec(memory_space=pltpu.HBM)
    shape = jax.ShapeDtypeStruct(pair_rep.shape, BF16)
    width = ns * 32
    nz = nd // 4
    args = (pair_rep, cotangent, residue_mask[None, :], w_proj, w_gate, w_out)
    args = [pltpu.with_memory_space_constraint(a, pltpu.HBM) for a in args]
    results = pl.pallas_call(
        functools.partial(kernel, nd, ns),
        out_shape=(shape, shape),
        in_specs=[hbm] * 6,
        out_specs=(vmem, vmem),
        scratch_shapes=[pltpu.VMEM(a.shape, a.dtype) for a in args]
        + [
            pltpu.VMEM((2, 16, 32, chans), BF16),
            pltpu.VMEM((8, nd * 16), F32),
            pltpu.VMEM((4, hidden, CELLS), F32),
            pltpu.VMEM((chans, CELLS), F32),
            pltpu.VMEM((chans, CELLS), F32),
            pltpu.VMEM((chans, CELLS), F32),
            pltpu.VMEM((hidden, CELLS), F32),
            pltpu.VMEM((chans, CELLS), BF16),
            pltpu.VMEM((QUADS, 16 * nz, 128), F32),
            pltpu.VMEM((4, ns, nz, CELLS), BF16),
            pltpu.VMEM((4, ns, nz, CELLS), BF16),
            pltpu.VMEM((2, nz, 16, width), BF16),
            pltpu.VMEM((2, nz, 16, width), BF16),
            pltpu.VMEM((3, nd, 16, width), BF16),
            pltpu.VMEM((3, nd, 16, width), BF16),
            pltpu.VMEM((2, nz, ns, CELLS), BF16),
            pltpu.VMEM((2, nz, ns, CELLS), BF16),
            pltpu.VMEM((ns, nz, CELLS), BF16),
            pltpu.VMEM((ns, nz, CELLS), BF16),
            pltpu.VMEM((4 * ns, nz, CELLS), BF16),
            pltpu.VMEM((4 * ns, nz, CELLS), BF16),
            pltpu.SemaphoreType.DMA((6,)),
            pltpu.SemaphoreType.DMA((12,)),
            pltpu.SemaphoreType.DMA((16,)),
        ],
        compiler_params=pltpu.CompilerParams(
            collective_id=0, has_side_effects=True, vmem_limit_bytes=50331648
        ),
    )(*args)
    return pl.pallas_call(
        to_hbm,
        out_shape=(shape, shape),
        in_specs=[vmem, vmem],
        out_specs=(hbm, hbm),
        scratch_shapes=[pltpu.SemaphoreType.DMA((2,))],
        compiler_params=pltpu.CompilerParams(vmem_limit_bytes=1024 * 1024),
    )(*results)


def solution(mesh):
    nd, ns = mesh.shape["dap"], mesh.shape["ch"]
    return jax.shard_map(
        functools.partial(on_device, nd, ns),
        mesh=mesh,
        in_specs=(P("dap", "ch", None), P(), P(), P(), P(), P("dap", "ch", None)),
        out_specs=(P("dap", "ch", None), P("dap", "ch", None)),
        check_vma=False,
    )
```

time: 75 us -> 70.7 us (0.943)
  Pallas kernels: 74.2 us -> 69.9 us
    pallas_call x1, Pallas kernels: 73.5 us -> 69.2 us  [on_device(): pl.pallas_call(functools.partial(kernel, nd, ns), out_shape=(shape, shape...]
where the time goes in v3:
time: 70.7 us; the launch traced here: 70.5 us
  Pallas kernels  69.9 us (99%)
    pallas_call x1, Pallas kernels, on_device(): pl.pallas_call(functools.partial(kernel, nd, ns), out_shape=(shape, shape...  69.2 us

profile of v3, /device:TPU:1, one launch (start us, length us, event | category | flops | bytes accessed | tf_op | source)
XLA Modules:
  0.0 70.5 jit_solution(872596078101618796)
XLA Ops:
  0.6 69.2 %shard_map.77 = (bf16[15,30,128]{2,1,0:T(8,128)(2,1)S(1)}, bf16[15,30,128]{2,1,0:T(8,128)(2,1)S(1)}) custom-call(bf16[15,30,128]{2,1,0:T(8,128)(2,1)} %x_hbm.1, bf16[15,30,128]{2,1,0:T(8,128)(2,1)} %cot_hbm.1, s32[1,480]{1,0:T(1,128)} %bitcast.1, bf16[128,512]{1,0:T(8,128)(2,1)} %wp_hbm.1, bf16[128,128]{1,0:T(8,128)(2,1)} %wg_hbm.1, bf16[128,128]{1,0:T(8,128)(2,1)} %wo_hbm.1), custom_call_target="tpu_custom_call" | custom-call | tf_op jit(solution)/shard_map/pallas_call | solution.py:546
  69.8 0.7 %shard_map.78 = (bf16[15,30,128]{2,1,0:T(8,128)(2,1)}, bf16[15,30,128]{2,1,0:T(8,128)(2,1)}) custom-call(bf16[15,30,128]{2,1,0:T(8,128)(2,1)S(1)} %get-tuple-element.4.upd, bf16[15,30,128]{2,1,0:T(8,128)(2,1)S(1)} %get-tuple-element.5.gpair), custom_call_target="tpu_custom_call" | custom-call | tf_op jit(solution)/shard_map/pallas_call | solution.py:582

commit v4 on v3

--- a/solution.py
+++ b/solution.py
@@ -12,6 +12,8 @@
 BF16 = jnp.bfloat16
 CELLS = 512
 QUADS = CELLS // 128
+LEFT, RIGHT, PRODUCT, GRAD, GRAD_LEFT, GRAD_RIGHT = range(6)
+BY_Z = (RIGHT, GRAD_RIGHT)
 
 
 def ring_order(size):
@@ -119,8 +121,11 @@
     z_in,
     col_out,
     col_in,
-    own_cells_in,
-    own_cells_out,
+    own_cells,
+    cell_tiles,
+    own_tiles,
+    own_mid,
+    flat,
     load_sem,
     send_sem,
     recv_sem,
@@ -223,26 +228,20 @@
         def _():
             await_slabs(ref, ref.shape[0], sem)
 
-    def across_ch(n, sem):
-        src, dst = ch_out.at[n], ch_in.at[n]
+    def across_ch(n):
+        src, dst, sem = ch_out.at[n], ch_in.at[n], 8 * n
         for s in near_ch:
             push(src.at[s], dst.at[me_s], sem, {"ch": s}).start()
         dst[me_s] = src[me_s]
 
-    def await_ch(n, sem):
-        await_slabs(ch_in.at[n], ns - 1, sem)
-
-    def across_z(n, sem):
-        src, dst = z_out.at[n], z_in.at[n]
+    def across_z(n):
+        src, dst, sem = z_out.at[n], z_in.at[n], 8 * n
         for z in z_order[:-1]:
             push(src.at[z], dst.at[my_z], sem, {"dap": at_dap(my_x, z, my_core)}).start()
         dst[my_z] = src[my_z]
 
-    def await_z(n, sem):
-        await_slabs(z_in.at[n], nz - 1, sem)
-
-    def rows_to_owners(n, a, sem):
-        src, dst = row_out.at[n], own_in.at[a]
+    def rows_to_owners(n, a):
+        src, dst, sem = row_out.at[n], own_in.at[a], 8 * n + 1
 
         def send(z):
             push(src.at[z], dst.at[me_d], sem, {"dap": owner_of(z, me_s)}).start()
@@ -258,24 +257,250 @@
         def _():
             send(my_z)
 
-    def columns_to_owners(sem):
+    def columns_to_owners(n):
         quarter = 2 * my_x + my_core
         slot = quarter * ns + me_s
+        sem = 8 * n + 1
 
         def send(s):
             peer = {"dap": owner_of(my_z, s), "ch": s}
-            push(col_out.at[s], own_cells_in.at[slot], sem, peer, 12 + quarter).start()
+            push(col_out.at[n, s], own_cells.at[n, slot], sem, peer, sem + quarter).start()
 
         for s in near_ch:
             send(s)
 
         @pl.when(is_owner)
         def _():
-            own_cells_in[slot] = col_out[me_s]
+            own_cells[n, slot] = col_out[n, me_s]
 
         @pl.when(jnp.logical_not(is_owner))
         def _():
             send(me_s)
+
+    def leave(n, value):
+        if n in BY_Z:
+            for q in range(QUADS):
+                lanes = slice(q * 128, q * 128 + 128)
+                mid[q, 0:hidden, :] = value[:, lanes]
+                for z in range(nz):
+                    z_out[n, z, :, lanes] = mid[q, pl.ds(z, ns, stride=nz), :].astype(BF16)
+        else:
+            ch_out[n] = value.reshape(ns, nz, CELLS).astype(BF16)
+
+    def across(n):
+        if n in BY_Z:
+            across_z(n)
+        else:
+            across_ch(n)
+
+    def forward(n, a):
+        if n in BY_Z:
+            await_slabs(z_in.at[n], nz - 1, 8 * n)
+            swap_leading(z_in.at[n], mid, col_out.at[n])
+            columns_to_owners(n)
+        else:
+            await_slabs(ch_in.at[n], ns - 1, 8 * n)
+            cells_to_rows(ch_in.at[n], 0, ns, mid, row_out.at[n], lambda m: m)
+            rows_to_owners(n, a)
+
+    def gathered(n, a):
+        if n not in BY_Z:
+            await_slabs(own_in.at[a], nd - 1, 8 * n + 1)
+            return
+
+        def arrived(x, core, count):
+            quarter = 2 * x + core
+            await_slabs(own_cells.at[n], count, 8 * n + 1 + quarter)
+            cells_to_rows(
+                own_cells.at[n],
+                quarter * ns,
+                ns,
+                mid,
+                own_in.at[a],
+                lambda z: at_dap(x, z, core),
+            )
+
+        arrived(my_x, 1, ns - 1)
+
+        @pl.loop(0, 3)
+        def _(r):
+            arrived(jnp.where(r == 0, my_x, other_x), lax.rem(r, 2), ns)
+
+    def multiply(a, b, contract, c):
+        right = own_in[b].reshape(many, width)
+        for h in range(2):
+            if contract[0][0] == 1:
+                part = own_in[a, pl.ds(h * nd // 2, nd // 2)].reshape(many // 2, width)
+            else:
+                part = own_in[a, :, :, pl.ds(h * width // 2, width // 2)].reshape(many, width // 2)
+            value = dot(part, right, contract)
+            if c is None:
+                for t in range(ns // 4):
+                    own_mid[t, pl.ds(h * many // 2, many // 2), :] = value[:, t * 128 : t * 128 + 128]
+            else:
+                value = value.astype(BF16).reshape(nd // 2, 16, width)
+                own_out[c, pl.ds(h * nd // 2, nd // 2)] = value
+
+    tiles = ns // 4
+    my_tile = me_s // 4
+    me = me_d * ns + me_s
+
+    def tile_at(step):
+        shift = jnp.where(lax.rem(step, 2) == 1, -((step + 1) // 2), step // 2)
+        return lax.rem(my_tile + tiles // 2 + shift, tiles)
+
+    def scatter_product():
+        mine = me_s * nz + my_z
+
+        @pl.loop(0, tiles)
+        def _(step):
+            t = tile_at(step)
+            for p in range(nd // 2):
+                moved = swap_blocks([own_mid[t, pl.ds(32 * p + b, 8, stride=4), :] for b in range(4)])
+                for a in range(4):
+                    line = moved[a].astype(BF16)
+                    for core in range(2):
+                        own_tiles[0, (2 * p + core) * ns + 4 * t + a] = line[
+                            4 * core : 4 * core + 4
+                        ]
+            for d in dap_order + [me_d]:
+                for a in range(4):
+                    s = 4 * t + a
+
+                    def send(d=d, s=s):
+                        push(
+                            own_tiles.at[0, d * ns + s],
+                            cell_tiles.at[0, mine],
+                            8 * PRODUCT,
+                            {"dap": d, "ch": s},
+                        ).start()
+
+                    if d is me_d:
+                        pl.when(s != me_s)(send)
+                    else:
+                        send()
+
+        cell_tiles[0, mine] = own_tiles[0, me]
+
+    def product_at_cells():
+        await_all_but_mine(cell_tiles.at[0], 8 * PRODUCT)
+
+        for c in range(hidden):
+            flat[pl.ds(4 * c, 4), :] = cell_tiles[0, c].astype(F32)
+
+        return jnp.concatenate(
+            [flat[pl.ds(q, hidden, stride=QUADS), :] for q in range(QUADS)], axis=1
+        )
+
+    def send_gradient(value):
+        for q in range(QUADS):
+            flat[pl.ds(q, hidden, stride=QUADS), :] = value[:, q * 128 : q * 128 + 128]
+
+        for c in range(hidden // 2):
+            pair = flat[pl.ds(8 * c, 8), :].astype(BF16)
+            cell_tiles[1, 2 * c] = pair[0:4]
+            cell_tiles[1, 2 * c + 1] = pair[4:8]
+
+        ny = ns // 2
+        steps = [(dz, dy, dx) for dz in range(nz) for dy in range(ny) for dx in range(2)]
+        steps.sort(key=lambda p: -(min(p[0], nz - p[0]) + min(p[1], ny - p[1]) + 2 * p[2]))
+        for dz, dy, dx in steps:
+            z = lax.rem(my_z + dz, nz)
+            s = 2 * lax.rem(me_s // 2 + dy, ny) + lax.rem(me_s + dx, 2)
+
+            def send(z=z, s=s):
+                push(
+                    cell_tiles.at[1, s * nz + z],
+                    own_tiles.at[1, me],
+                    8 * GRAD,
+                    {"dap": owner_of(z, s), "ch": s},
+                    8 * GRAD + 1 + my_tile,
+                ).start()
+
+            if dz or dy or dx:
+                send()
+            else:
+                pl.when(jnp.logical_not(is_owner))(send)
+
+        @pl.when(is_owner)
+        def _():
+            own_tiles[1, me] = cell_tiles[1, me_s * nz + my_z]
+
+    def gather_gradient(a):
+        @pl.loop(0, tiles)
+        def _(step):
+            t = tile_at(tiles - 1 - step)
+
+            def arrived(count):
+                some = own_tiles.at[1, pl.ds(0, count)]
+                push(some, some, 8 * GRAD, {"dap": me_d}, 8 * GRAD + 1 + t).wait_recv()
+
+            pl.when(t == my_tile)(lambda: arrived(4 * nd - 1))
+            pl.when(t != my_tile)(lambda: arrived(4 * nd))
+            for p in range(nd // 2):
+                got = [
+                    jnp.concatenate(
+                        [
+                            own_tiles[1, (2 * p + core) * ns + 4 * t + e].astype(F32)
+                            for core in range(2)
+                        ],
+                        axis=0,
+                    )
+                    for e in range(4)
+                ]
+                for b, rows in enumerate(swap_blocks(got)):
+                    own_mid[t, pl.ds(32 * p + b, 8, stride=4), :] = rows
+            lanes = pl.ds(pl.multiple_of(t * 128, 128), 128)
+            for d in range(nd):
+                own_in[a, d, :, lanes] = own_mid[t, pl.ds(16 * d, 16), :].astype(BF16)
+
+    def give_back(n, c):
+        if n not in BY_Z:
+            src, dst = own_out.at[c], row_in.at[n]
+            for d in dap_order:
+                push(src.at[d], dst.at[my_z], 8 * n + 1, {"dap": d}).start()
+            dst[my_z] = src[me_d]
+            return
+        for g, (x, core) in enumerate(quarters):
+            rows_to_cells(
+                own_out.at[c],
+                lambda z, x=x, core=core: at_dap(x, z, core),
+                mid,
+                own_cells.at[n],
+                g * ns,
+                ns,
+            )
+            d = at_dap(x, my_z, core)
+            for s in near_ch + ([me_s] if g < 3 else []):
+                push(
+                    own_cells.at[n, g * ns + s],
+                    col_in.at[n, me_s],
+                    8 * n + 1,
+                    {"dap": d, "ch": s},
+                ).start()
+        col_in[n, me_s] = own_cells[n, 3 * ns + me_s]
+
+    def pass_on(n):
+        if n in BY_Z:
+            await_all_but_mine(col_in.at[n], 8 * n + 1)
+            swap_leading(col_in.at[n], mid, z_out.at[n])
+        else:
+            await_all_but_mine(row_in.at[n], 8 * n + 1)
+            rows_to_cells(row_in.at[n], lambda m: m, mid, ch_out.at[n], 0, ns)
+        across(n)
+
+    def arrive(n):
+        if n not in BY_Z:
+            await_slabs(ch_in.at[n], ns - 1, 8 * n)
+            return ch_in[n].reshape(hidden, CELLS).astype(F32)
+        await_slabs(z_in.at[n], nz - 1, 8 * n)
+        for q in range(QUADS):
+            for z in range(nz):
+                mid[q, pl.ds(z, ns, stride=nz), :] = z_in[n, z, :, pl.ds(q * 128, 128)].astype(F32)
+        return jnp.concatenate([mid[q, 0:hidden, :] for q in range(QUADS)], axis=1)
+
+    width = ns * 32
+    many = nd * 16
 
     lane = lax.broadcasted_iota(jnp.int32, (1, CELLS), 1)
     place = lax.rem(lane, 16)
@@ -347,16 +572,11 @@
         return sig * val * mask
 
     loads[1].wait()
-    ch_out[0] = edge(0).reshape(ns, nz, CELLS).astype(BF16)
-    right = edge(2)
-    for q in range(QUADS):
-        lanes = slice(q * 128, q * 128 + 128)
-        mid[q, 0:hidden, :] = right[:, lanes]
-        for z in range(nz):
-            z_out[0, z, :, lanes] = mid[q, pl.ds(z, ns, stride=nz), :].astype(BF16)
+    leave(LEFT, edge(0))
+    leave(RIGHT, edge(2))
     pl.semaphore_wait(barrier, greetings)
-    across_z(0, 1)
-    across_ch(0, 0)
+    across(RIGHT)
+    across(LEFT)
 
     for load in loads[3:]:
         load.wait()
@@ -367,104 +587,37 @@
     gh = dot(wo_ref[...], (ct * gv).astype(BF16), ((1,), (0,)))
     ghid[...] = gh - jnp.mean(gh, axis=0, keepdims=True)
 
-    await_z(0, 1)
-    swap_leading(z_in.at[0], mid, col_out)
-    columns_to_owners(3)
-    await_ch(0, 0)
-    cells_to_rows(ch_in.at[0], 0, ns, mid, row_out.at[0], lambda m: m)
-    rows_to_owners(0, 0, 2)
-
-    width = ns * 32
-    many = nd * 16
-
-    def multiply(a, b, contract, n):
-        right = own_in[b].reshape(many, width)
-        for h in range(2):
-            if contract[0][0] == 1:
-                part = own_in[a, pl.ds(h * nd // 2, nd // 2)].reshape(many // 2, width)
-            else:
-                part = own_in[a, :, :, pl.ds(h * width // 2, width // 2)].reshape(many, width // 2)
-            value = dot(part, right, contract).astype(BF16)
-            own_out[n, pl.ds(h * nd // 2, nd // 2)] = value.reshape(nd // 2, 16, width)
-
-    def rows_back(n, sem):
-        src, dst = own_out.at[n], row_in.at[n]
-        for d in dap_order:
-            push(src.at[d], dst.at[my_z], sem, {"dap": d}).start()
-        dst[my_z] = src[me_d]
-
-    def columns_back(n, sem):
-        for g, (x, core) in enumerate(quarters):
-            rows_to_cells(
-                own_out.at[n],
-                lambda z, x=x, core=core: at_dap(x, z, core),
-                mid,
-                own_cells_out,
-                g * ns,
-                ns,
-            )
-            d = at_dap(x, my_z, core)
-            for s in near_ch + ([me_s] if g < 3 else []):
-                push(
-                    own_cells_out.at[g * ns + s], col_in.at[me_s], sem, {"dap": d, "ch": s}
-                ).start()
-        col_in[me_s] = own_cells_out[3 * ns + me_s]
+    forward(RIGHT, 1)
+    forward(LEFT, 0)
 
     @pl.when(is_owner)
     def _():
-        def arrived(x, core, count):
-            quarter = 2 * x + core
-            await_slabs(own_cells_in, count, 12 + quarter)
-            cells_to_rows(
-                own_cells_in,
-                quarter * ns,
-                ns,
-                mid,
-                own_in.at[1],
-                lambda z: at_dap(x, z, core),
-            )
-
-        arrived(my_x, 1, ns - 1)
-
-        @pl.loop(0, 3)
-        def _(r):
-            arrived(jnp.where(r == 0, my_x, other_x), lax.rem(r, 2), ns)
-
-        await_slabs(own_in.at[0], nd - 1, 2)
-        multiply(0, 1, ((1,), (1,)), 0)
-        rows_back(0, 4)
-
-    await_all_but_mine(row_in.at[0], 4)
-    rows_to_cells(row_in.at[0], lambda m: m, mid, ch_out.at[1], 0, ns)
-    across_ch(1, 5)
-    await_ch(1, 5)
-
-    prod = ch_in[1].reshape(hidden, CELLS).astype(F32)
+        gathered(RIGHT, 1)
+        gathered(LEFT, 0)
+        multiply(0, 1, ((1,), (1,)), None)
+        scatter_product()
+
+    prod = product_at_cells()
     away = prod - jnp.mean(prod, axis=0, keepdims=True)
     hidden_scale = lax.rsqrt(jnp.mean(away * away, axis=0, keepdims=True) + EPSILON)
     hn = away * hidden_scale
     gh_away = ghid[...]
     second = jnp.mean((gh_away) * hn, axis=0, keepdims=True)
     gprod = hidden_scale * (gh_away - hn * second)
-    ch_out[2] = gprod.reshape(ns, nz, CELLS).astype(BF16)
-    across_ch(2, 6)
+    send_gradient(gprod)
 
     po = dot(wo_ref[...], hn.astype(BF16), ((0,), (0,)))
     gv = gate[...]
     glogit[...] = (cot[...] * po * gv * (1.0 - gv)).astype(BF16)
     upd_ref[...] = cells_last(gv * po)
 
-    await_ch(2, 6)
-    cells_to_rows(ch_in.at[2], 0, ns, mid, row_out.at[1], lambda m: m)
-    rows_to_owners(1, 2, 7)
-
     @pl.when(is_owner)
     def _():
-        await_slabs(own_in.at[2], nd - 1, 7)
-        multiply(2, 1, ((1,), (0,)), 1)
-        rows_back(1, 8)
-        multiply(2, 0, ((0,), (0,)), 2)
-        columns_back(2, 9)
+        gather_gradient(2)
+        multiply(2, 1, ((1,), (0,)), 0)
+        give_back(GRAD_LEFT, 0)
+        multiply(2, 0, ((0,), (0,)), 1)
+        give_back(GRAD_RIGHT, 1)
 
     base = dot(wg_ref[...], glogit[...], ((1,), (0,)))
 
@@ -477,21 +630,10 @@
         base = base + dot(wp_ref[:, pl.ds(part * hidden, hidden)], to_sig, ((1,), (0,)))
         return base + dot(wp_ref[:, pl.ds((part + 1) * hidden, hidden)], to_val, ((1,), (0,)))
 
-    await_all_but_mine(row_in.at[1], 8)
-    rows_to_cells(row_in.at[1], lambda m: m, mid, ch_out.at[3], 0, ns)
-    across_ch(3, 10)
-    await_all_but_mine(col_in, 9)
-    swap_leading(col_in, mid, z_out.at[1])
-    across_z(1, 11)
-    await_ch(3, 10)
-    base = through(base, 0, ch_in[3].reshape(hidden, CELLS).astype(F32))
-    await_z(1, 11)
-    for q in range(QUADS):
-        lanes = slice(q * 128, q * 128 + 128)
-        for z in range(nz):
-            mid[q, pl.ds(z, ns, stride=nz), :] = z_in[1, z, :, lanes].astype(F32)
-    back = jnp.concatenate([mid[q, 0:hidden, :] for q in range(QUADS)], axis=1)
-    base = through(base, 2, back)
+    pass_on(GRAD_LEFT)
+    pass_on(GRAD_RIGHT)
+    base = through(base, 0, arrive(GRAD_LEFT))
+    base = through(base, 2, arrive(GRAD_RIGHT))
 
     nt = normed[...]
     first = jnp.mean(base, axis=0, keepdims=True)
@@ -502,25 +644,37 @@
         some = ref.at[pl.ds(0, count)]
         push(some, some, sem, {"dap": me_d}).wait_send()
 
-    for n, sem in ((0, 0), (1, 5), (2, 6), (3, 10)):
-        sent(ch_out.at[n], ns - 1, sem)
-    for n, sem in ((0, 1), (1, 11)):
-        sent(z_out.at[n], nz - 1, sem)
+    inward = (LEFT, RIGHT)
+    outward = (GRAD_LEFT, GRAD_RIGHT)
+    for n in inward + outward:
+        if n in BY_Z:
+            sent(z_out.at[n], nz - 1, 8 * n)
+        else:
+            sent(ch_out.at[n], ns - 1, 8 * n)
 
     @pl.when(is_owner)
     def _():
-        sent(row_out.at[0], nz - 1, 2)
-        sent(row_out.at[1], nz - 1, 7)
-        sent(col_out, ns - 1, 3)
-        sent(own_out.at[0], nd - 1, 4)
-        sent(own_out.at[1], nd - 1, 8)
-        sent(own_cells_out, 4 * ns - 1, 9)
+        sent(own_tiles.at[0], nd * ns - 1, 8 * PRODUCT)
+        sent(cell_tiles.at[1], ns * nz - 1, 8 * GRAD)
+        for n in inward:
+            if n in BY_Z:
+                sent(col_out.at[n], ns - 1, 8 * n + 1)
+            else:
+                sent(row_out.at[n], nz - 1, 8 * n + 1)
+        for c, n in enumerate(outward):
+            if n in BY_Z:
+                sent(own_cells.at[n], 4 * ns - 1, 8 * n + 1)
+            else:
+                sent(own_out.at[c], nd - 1, 8 * n + 1)
 
     @pl.when(jnp.logical_not(is_owner))
     def _():
-        sent(row_out.at[0], nz, 2)
-        sent(row_out.at[1], nz, 7)
-        sent(col_out, ns, 3)
+        sent(cell_tiles.at[1], ns * nz, 8 * GRAD)
+        for n in inward:
+            if n in BY_Z:
+                sent(col_out.at[n], ns, 8 * n + 1)
+            else:
+                sent(row_out.at[n], nz, 8 * n + 1)
 
 
 def to_hbm(upd, gpair, upd_hbm, gpair_hbm, sem):
@@ -559,21 +713,24 @@
             pltpu.VMEM((hidden, CELLS), F32),
             pltpu.VMEM((chans, CELLS), BF16),
             pltpu.VMEM((QUADS, 16 * nz, 128), F32),
-            pltpu.VMEM((4, ns, nz, CELLS), BF16),
-            pltpu.VMEM((4, ns, nz, CELLS), BF16),
-            pltpu.VMEM((2, nz, 16, width), BF16),
-            pltpu.VMEM((2, nz, 16, width), BF16),
+            pltpu.VMEM((6, ns, nz, CELLS), BF16),
+            pltpu.VMEM((6, ns, nz, CELLS), BF16),
+            pltpu.VMEM((6, nz, 16, width), BF16),
+            pltpu.VMEM((6, nz, 16, width), BF16),
             pltpu.VMEM((3, nd, 16, width), BF16),
             pltpu.VMEM((3, nd, 16, width), BF16),
-            pltpu.VMEM((2, nz, ns, CELLS), BF16),
-            pltpu.VMEM((2, nz, ns, CELLS), BF16),
-            pltpu.VMEM((ns, nz, CELLS), BF16),
-            pltpu.VMEM((ns, nz, CELLS), BF16),
-            pltpu.VMEM((4 * ns, nz, CELLS), BF16),
-            pltpu.VMEM((4 * ns, nz, CELLS), BF16),
+            pltpu.VMEM((6, nz, ns, CELLS), BF16),
+            pltpu.VMEM((6, nz, ns, CELLS), BF16),
+            pltpu.VMEM((6, ns, nz, CELLS), BF16),
+            pltpu.VMEM((6, ns, nz, CELLS), BF16),
+            pltpu.VMEM((6, 4 * ns, nz, CELLS), BF16),
+            pltpu.VMEM((2, ns * nz, QUADS, 128), BF16),
+            pltpu.VMEM((2, nd * ns, QUADS, 128), BF16),
+            pltpu.VMEM((ns // 4, nd * 16, 128), F32),
+            pltpu.VMEM((QUADS * ns * nz, 128), F32),
             pltpu.SemaphoreType.DMA((6,)),
-            pltpu.SemaphoreType.DMA((12,)),
-            pltpu.SemaphoreType.DMA((16,)),
+            pltpu.SemaphoreType.DMA((48,)),
+            pltpu.SemaphoreType.DMA((48,)),
         ],
         compiler_params=pltpu.CompilerParams(
             collective_id=0, has_side_effects=True, vmem_limit_bytes=50331648

time: 70.7 us -> 64.9 us (0.918)
  Pallas kernels: 69.9 us -> 64.1 us
    pallas_call x1, Pallas kernels: 69.2 us -> 63.4 us  [on_device(): pl.pallas_call(functools.partial(kernel, nd, ns), out_shape=(shape, shape...]
where the time goes in v4:
time: 64.9 us; the launch traced here: 64.8 us
  Pallas kernels  64.1 us (99%)
    pallas_call x1, Pallas kernels, on_device(): pl.pallas_call(functools.partial(kernel, nd, ns), out_shape=(shape, shape...  63.4 us

profile of v4, /device:TPU:1, one launch (start us, length us, event | category | flops | bytes accessed | tf_op | source)
XLA Modules:
  0.0 64.8 jit_solution(10992330485969582814)
XLA Ops:
  0.6 63.4 %shard_map.77 = (bf16[15,30,128]{2,1,0:T(8,128)(2,1)S(1)}, bf16[15,30,128]{2,1,0:T(8,128)(2,1)S(1)}) custom-call(bf16[15,30,128]{2,1,0:T(8,128)(2,1)} %x_hbm.1, bf16[15,30,128]{2,1,0:T(8,128)(2,1)} %cot_hbm.1, s32[1,480]{1,0:T(1,128)} %bitcast.1, bf16[128,512]{1,0:T(8,128)(2,1)} %wp_hbm.1, bf16[128,128]{1,0:T(8,128)(2,1)} %wg_hbm.1, bf16[128,128]{1,0:T(8,128)(2,1)} %wo_hbm.1), custom_call_target="tpu_custom_call" | custom-call | tf_op jit(solution)/shard_map/pallas_call | solution.py:700
  64.1 0.7 %shard_map.78 = (bf16[15,30,128]{2,1,0:T(8,128)(2,1)}, bf16[15,30,128]{2,1,0:T(8,128)(2,1)}) custom-call(bf16[15,30,128]{2,1,0:T(8,128)(2,1)S(1)} %get-tuple-element.4.upd, bf16[15,30,128]{2,1,0:T(8,128)(2,1)S(1)} %get-tuple-element.5.gpair), custom_call_target="tpu_custom_call" | custom-call | tf_op jit(solution)/shard_map/pallas_call | solution.py:739

commit v5 on v4

--- a/solution.py
+++ b/solution.py
@@ -12,8 +12,9 @@
 BF16 = jnp.bfloat16
 CELLS = 512
 QUADS = CELLS // 128
-LEFT, RIGHT, PRODUCT, GRAD, GRAD_LEFT, GRAD_RIGHT = range(6)
-BY_Z = (RIGHT, GRAD_RIGHT)
+LEFT, RIGHT, PRODUCT, GRAD, GRADS = range(5)
+ARRIVALS = 40
+BY_Z = (RIGHT,)
 
 
 def ring_order(size):
@@ -60,19 +61,6 @@
     for t in range(count // 4):
         for m in range(group):
             rows[place(m), :, pl.ds(t * 128, 128)] = mid[t, pl.ds(16 * m, 16), :].astype(BF16)
-
-
-def rows_to_cells(rows, place, mid, cells, first, count):
-    group = cells.shape[1]
-    for t in range(count // 4):
-        for m in range(group):
-            mid[t, pl.ds(16 * m, 16), :] = rows[place(m), :, pl.ds(t * 128, 128)].astype(F32)
-    for t in range(count // 4):
-        for q in range(QUADS):
-            lanes = pl.ds(q * 128, 128)
-            moved = swap_blocks([mid[t, pl.ds(4 * q + b, group, stride=16), :] for b in range(4)])
-            for a in range(4):
-                cells[first + 4 * t + a, :, lanes] = moved[a].astype(BF16)
 
 
 def swap_leading(src, mid, dst):
@@ -114,16 +102,17 @@
     ch_out,
     ch_in,
     row_out,
-    row_in,
     own_in,
-    own_out,
     z_out,
     z_in,
     col_out,
-    col_in,
     own_cells,
-    cell_tiles,
-    own_tiles,
+    prod_cell,
+    prod_own,
+    grad_cell,
+    grad_own,
+    grads_cell,
+    grads_own,
     own_mid,
     flat,
     load_sem,
@@ -326,22 +315,20 @@
         def _(r):
             arrived(jnp.where(r == 0, my_x, other_x), lax.rem(r, 2), ns)
 
-    def multiply(a, b, contract, c):
+    width = ns * 32
+    many = nd * 16
+    tiles = ns // 4
+
+    def multiply(a, b, contract, k, h):
         right = own_in[b].reshape(many, width)
-        for h in range(2):
-            if contract[0][0] == 1:
-                part = own_in[a, pl.ds(h * nd // 2, nd // 2)].reshape(many // 2, width)
-            else:
-                part = own_in[a, :, :, pl.ds(h * width // 2, width // 2)].reshape(many, width // 2)
-            value = dot(part, right, contract)
-            if c is None:
-                for t in range(ns // 4):
-                    own_mid[t, pl.ds(h * many // 2, many // 2), :] = value[:, t * 128 : t * 128 + 128]
-            else:
-                value = value.astype(BF16).reshape(nd // 2, 16, width)
-                own_out[c, pl.ds(h * nd // 2, nd // 2)] = value
-
-    tiles = ns // 4
+        if contract[0][0] == 1:
+            part = own_in[a, pl.ds(h * nd // 2, nd // 2)].reshape(many // 2, width)
+        else:
+            part = own_in[a, :, :, pl.ds(h * width // 2, width // 2)].reshape(many, width // 2)
+        value = dot(part, right, contract)
+        for t in range(tiles):
+            own_mid[k, t, pl.ds(h * many // 2, many // 2), :] = value[:, t * 128 : t * 128 + 128]
+
     my_tile = me_s // 4
     me = me_d * ns + me_s
 
@@ -349,57 +336,59 @@
         shift = jnp.where(lax.rem(step, 2) == 1, -((step + 1) // 2), step // 2)
         return lax.rem(my_tile + tiles // 2 + shift, tiles)
 
-    def scatter_product():
+    def tiles_back(own, cell, sem, h, kinds, whole):
         mine = me_s * nz + my_z
 
         @pl.loop(0, tiles)
         def _(step):
             t = tile_at(step)
-            for p in range(nd // 2):
-                moved = swap_blocks([own_mid[t, pl.ds(32 * p + b, 8, stride=4), :] for b in range(4)])
-                for a in range(4):
-                    line = moved[a].astype(BF16)
-                    for core in range(2):
-                        own_tiles[0, (2 * p + core) * ns + 4 * t + a] = line[
-                            4 * core : 4 * core + 4
-                        ]
-            for d in dap_order + [me_d]:
-                for a in range(4):
-                    s = 4 * t + a
-
-                    def send(d=d, s=s):
-                        push(
-                            own_tiles.at[0, d * ns + s],
-                            cell_tiles.at[0, mine],
-                            8 * PRODUCT,
-                            {"dap": d, "ch": s},
-                        ).start()
-
-                    if d is me_d:
-                        pl.when(s != me_s)(send)
-                    else:
-                        send()
-
-        cell_tiles[0, mine] = own_tiles[0, me]
-
-    def product_at_cells():
-        await_all_but_mine(cell_tiles.at[0], 8 * PRODUCT)
-
-        for c in range(hidden):
-            flat[pl.ds(4 * c, 4), :] = cell_tiles[0, c].astype(F32)
-
-        return jnp.concatenate(
-            [flat[pl.ds(q, hidden, stride=QUADS), :] for q in range(QUADS)], axis=1
-        )
-
-    def send_gradient(value):
+            for k in kinds:
+                for p in range(h * nz, h * nz + nz):
+                    moved = swap_blocks(
+                        [own_mid[k, t, pl.ds(32 * p + b, 8, stride=4), :] for b in range(4)]
+                    )
+                    for a in range(4):
+                        line = moved[a].astype(BF16)
+                        for core in range(2):
+                            own[(2 * p + core) * ns + 4 * t + a, k] = line[4 * core : 4 * core + 4]
+            for n, z in enumerate(z_order):
+                for core in range(2):
+                    d = at_dap(h, z, core)
+                    for a in range(4):
+                        s = 4 * t + a
+
+                        def send(d=d, s=s):
+                            src, dst = own.at[d * ns + s], cell.at[mine]
+                            if not whole:
+                                src, dst = src.at[kinds[0]], dst.at[kinds[0]]
+                            push(src, dst, sem, {"dap": d, "ch": s}).start()
+
+                        if n == nz - 1 and core == 1:
+                            pl.when(d * ns + s != me)(send)
+                        else:
+                            send()
+
+    def tiles_at_cells(cell, sem):
+        await_all_but_mine(cell, sem)
+        found = []
+        for k in range(cell.shape[1]):
+            for c in range(hidden):
+                flat[pl.ds(4 * c, 4), :] = cell[c, k].astype(F32)
+            found.append(
+                jnp.concatenate(
+                    [flat[pl.ds(q, hidden, stride=QUADS), :] for q in range(QUADS)], axis=1
+                )
+            )
+        return found
+
+    def tiles_to_owners(value):
+        n = GRAD
         for q in range(QUADS):
             flat[pl.ds(q, hidden, stride=QUADS), :] = value[:, q * 128 : q * 128 + 128]
-
         for c in range(hidden // 2):
             pair = flat[pl.ds(8 * c, 8), :].astype(BF16)
-            cell_tiles[1, 2 * c] = pair[0:4]
-            cell_tiles[1, 2 * c + 1] = pair[4:8]
+            grad_cell[2 * c] = pair[0:4]
+            grad_cell[2 * c + 1] = pair[4:8]
 
         ny = ns // 2
         steps = [(dz, dy, dx) for dz in range(nz) for dy in range(ny) for dx in range(2)]
@@ -410,11 +399,11 @@
 
             def send(z=z, s=s):
                 push(
-                    cell_tiles.at[1, s * nz + z],
-                    own_tiles.at[1, me],
-                    8 * GRAD,
+                    grad_cell.at[s * nz + z],
+                    grad_own.at[me],
+                    8 * n,
                     {"dap": owner_of(z, s), "ch": s},
-                    8 * GRAD + 1 + my_tile,
+                    ARRIVALS + 4 * my_x + my_tile,
                 ).start()
 
             if dz or dy or dx:
@@ -424,24 +413,25 @@
 
         @pl.when(is_owner)
         def _():
-            own_tiles[1, me] = cell_tiles[1, me_s * nz + my_z]
-
-    def gather_gradient(a):
+            grad_own[me] = grad_cell[me_s * nz + my_z]
+
+    def tiles_gathered(a, h):
         @pl.loop(0, tiles)
         def _(step):
             t = tile_at(tiles - 1 - step)
 
             def arrived(count):
-                some = own_tiles.at[1, pl.ds(0, count)]
-                push(some, some, 8 * GRAD, {"dap": me_d}, 8 * GRAD + 1 + t).wait_recv()
-
-            pl.when(t == my_tile)(lambda: arrived(4 * nd - 1))
-            pl.when(t != my_tile)(lambda: arrived(4 * nd))
-            for p in range(nd // 2):
+                some = grad_own.at[pl.ds(0, count)]
+                push(some, some, 8 * GRAD, {"dap": me_d}, ARRIVALS + 4 * h + t).wait_recv()
+
+            mine_too = jnp.logical_and(t == my_tile, my_x == h)
+            pl.when(mine_too)(lambda: arrived(2 * nd - 1))
+            pl.when(jnp.logical_not(mine_too))(lambda: arrived(2 * nd))
+            for p in range(h * nz, h * nz + nz):
                 got = [
                     jnp.concatenate(
                         [
-                            own_tiles[1, (2 * p + core) * ns + 4 * t + e].astype(F32)
+                            grad_own[(2 * p + core) * ns + 4 * t + e].astype(F32)
                             for core in range(2)
                         ],
                         axis=0,
@@ -449,58 +439,10 @@
                     for e in range(4)
                 ]
                 for b, rows in enumerate(swap_blocks(got)):
-                    own_mid[t, pl.ds(32 * p + b, 8, stride=4), :] = rows
+                    own_mid[0, t, pl.ds(32 * p + b, 8, stride=4), :] = rows
             lanes = pl.ds(pl.multiple_of(t * 128, 128), 128)
-            for d in range(nd):
-                own_in[a, d, :, lanes] = own_mid[t, pl.ds(16 * d, 16), :].astype(BF16)
-
-    def give_back(n, c):
-        if n not in BY_Z:
-            src, dst = own_out.at[c], row_in.at[n]
-            for d in dap_order:
-                push(src.at[d], dst.at[my_z], 8 * n + 1, {"dap": d}).start()
-            dst[my_z] = src[me_d]
-            return
-        for g, (x, core) in enumerate(quarters):
-            rows_to_cells(
-                own_out.at[c],
-                lambda z, x=x, core=core: at_dap(x, z, core),
-                mid,
-                own_cells.at[n],
-                g * ns,
-                ns,
-            )
-            d = at_dap(x, my_z, core)
-            for s in near_ch + ([me_s] if g < 3 else []):
-                push(
-                    own_cells.at[n, g * ns + s],
-                    col_in.at[n, me_s],
-                    8 * n + 1,
-                    {"dap": d, "ch": s},
-                ).start()
-        col_in[n, me_s] = own_cells[n, 3 * ns + me_s]
-
-    def pass_on(n):
-        if n in BY_Z:
-            await_all_but_mine(col_in.at[n], 8 * n + 1)
-            swap_leading(col_in.at[n], mid, z_out.at[n])
-        else:
-            await_all_but_mine(row_in.at[n], 8 * n + 1)
-            rows_to_cells(row_in.at[n], lambda m: m, mid, ch_out.at[n], 0, ns)
-        across(n)
-
-    def arrive(n):
-        if n not in BY_Z:
-            await_slabs(ch_in.at[n], ns - 1, 8 * n)
-            return ch_in[n].reshape(hidden, CELLS).astype(F32)
-        await_slabs(z_in.at[n], nz - 1, 8 * n)
-        for q in range(QUADS):
-            for z in range(nz):
-                mid[q, pl.ds(z, ns, stride=nz), :] = z_in[n, z, :, pl.ds(q * 128, 128)].astype(F32)
-        return jnp.concatenate([mid[q, 0:hidden, :] for q in range(QUADS)], axis=1)
-
-    width = ns * 32
-    many = nd * 16
+            for d in range(h * nd // 2, (h + 1) * nd // 2):
+                own_in[a, d, :, lanes] = own_mid[0, t, pl.ds(16 * d, 16), :].astype(BF16)
 
     lane = lax.broadcasted_iota(jnp.int32, (1, CELLS), 1)
     place = lax.rem(lane, 16)
@@ -525,15 +467,6 @@
             lax.rem(lane, 32) < half, turned, pltpu.roll(turned, CELLS - 1, 1)
         )
         return closed.T.reshape(16, 32, chans)[0:rows, 0:columns, :].astype(BF16)
-
-    loads[0].wait()
-    xt = cells_first(x_ref, 0)
-    center = jnp.mean(xt, axis=0, keepdims=True)
-    spread = xt - center
-    pair_scale = lax.rsqrt(jnp.mean(spread * spread, axis=0, keepdims=True) + EPSILON)
-    nt = spread * pair_scale
-    normed[...] = nt
-    nh = nt.astype(BF16)
 
     residues = mask_ref.shape[1]
     total = nd * 16
@@ -560,6 +493,15 @@
     col_mask = jnp.concatenate([col_flags] * (CELLS // 128), axis=1)
     mask = (row_mask * col_mask)[0:1]
 
+    loads[0].wait()
+    xt = cells_first(x_ref, 0)
+    center = jnp.mean(xt, axis=0, keepdims=True)
+    spread = xt - center
+    pair_scale = lax.rsqrt(jnp.mean(spread * spread, axis=0, keepdims=True) + EPSILON)
+    nt = spread * pair_scale
+    normed[...] = nt
+    nh = nt.astype(BF16)
+
     def project(part):
         raw = dot(wp_ref[:, pl.ds(part * hidden, hidden)], nh, ((0,), (0,)))
         return raw
@@ -594,17 +536,19 @@
     def _():
         gathered(RIGHT, 1)
         gathered(LEFT, 0)
-        multiply(0, 1, ((1,), (1,)), None)
-        scatter_product()
-
-    prod = product_at_cells()
+        for h in range(2):
+            multiply(0, 1, ((1,), (1,)), 0, h)
+            tiles_back(prod_own, prod_cell, 8 * PRODUCT, h, (0,), True)
+        prod_cell[me_s * nz + my_z] = prod_own[me]
+
+    (prod,) = tiles_at_cells(prod_cell, 8 * PRODUCT)
     away = prod - jnp.mean(prod, axis=0, keepdims=True)
     hidden_scale = lax.rsqrt(jnp.mean(away * away, axis=0, keepdims=True) + EPSILON)
     hn = away * hidden_scale
     gh_away = ghid[...]
     second = jnp.mean((gh_away) * hn, axis=0, keepdims=True)
     gprod = hidden_scale * (gh_away - hn * second)
-    send_gradient(gprod)
+    tiles_to_owners(gprod)
 
     po = dot(wo_ref[...], hn.astype(BF16), ((0,), (0,)))
     gv = gate[...]
@@ -613,11 +557,16 @@
 
     @pl.when(is_owner)
     def _():
-        gather_gradient(2)
-        multiply(2, 1, ((1,), (0,)), 0)
-        give_back(GRAD_LEFT, 0)
-        multiply(2, 0, ((0,), (0,)), 1)
-        give_back(GRAD_RIGHT, 1)
+        tiles_gathered(2, 0)
+        multiply(2, 1, ((1,), (0,)), 0, 0)
+        tiles_back(grads_own, grads_cell, 8 * GRADS, 0, (0,), False)
+        tiles_gathered(2, 1)
+        multiply(2, 1, ((1,), (0,)), 0, 1)
+        multiply(2, 0, ((0,), (0,)), 1, 1)
+        tiles_back(grads_own, grads_cell, 8 * GRADS, 1, (0, 1), True)
+        multiply(2, 0, ((0,), (0,)), 1, 0)
+        tiles_back(grads_own, grads_cell, 8 * GRADS, 0, (1,), False)
+        grads_cell[me_s * nz + my_z] = grads_own[me]
 
     base = dot(wg_ref[...], glogit[...], ((1,), (0,)))
 
@@ -630,10 +579,9 @@
         base = base + dot(wp_ref[:, pl.ds(part * hidden, hidden)], to_sig, ((1,), (0,)))
         return base + dot(wp_ref[:, pl.ds((part + 1) * hidden, hidden)], to_val, ((1,), (0,)))
 
-    pass_on(GRAD_LEFT)
-    pass_on(GRAD_RIGHT)
-    base = through(base, 0, arrive(GRAD_LEFT))
-    base = through(base, 2, arrive(GRAD_RIGHT))
+    back_left, back_right = tiles_at_cells(grads_cell, 8 * GRADS)
+    base = through(base, 0, back_left)
+    base = through(base, 2, back_right)
 
     nt = normed[...]
     first = jnp.mean(base, axis=0, keepdims=True)
@@ -644,37 +592,22 @@
         some = ref.at[pl.ds(0, count)]
         push(some, some, sem, {"dap": me_d}).wait_send()
 
-    inward = (LEFT, RIGHT)
-    outward = (GRAD_LEFT, GRAD_RIGHT)
-    for n in inward + outward:
-        if n in BY_Z:
-            sent(z_out.at[n], nz - 1, 8 * n)
-        else:
-            sent(ch_out.at[n], ns - 1, 8 * n)
+    sent(ch_out.at[LEFT], ns - 1, 8 * LEFT)
+    sent(z_out.at[RIGHT], nz - 1, 8 * RIGHT)
 
     @pl.when(is_owner)
     def _():
-        sent(own_tiles.at[0], nd * ns - 1, 8 * PRODUCT)
-        sent(cell_tiles.at[1], ns * nz - 1, 8 * GRAD)
-        for n in inward:
-            if n in BY_Z:
-                sent(col_out.at[n], ns - 1, 8 * n + 1)
-            else:
-                sent(row_out.at[n], nz - 1, 8 * n + 1)
-        for c, n in enumerate(outward):
-            if n in BY_Z:
-                sent(own_cells.at[n], 4 * ns - 1, 8 * n + 1)
-            else:
-                sent(own_out.at[c], nd - 1, 8 * n + 1)
+        sent(row_out.at[LEFT], nz - 1, 8 * LEFT + 1)
+        sent(col_out.at[RIGHT], ns - 1, 8 * RIGHT + 1)
+        sent(grad_cell, hidden - 1, 8 * GRAD)
+        sent(prod_own, nd * ns - 1, 8 * PRODUCT)
+        sent(grads_own, nd * ns - 1, 8 * GRADS)
 
     @pl.when(jnp.logical_not(is_owner))
     def _():
-        sent(cell_tiles.at[1], ns * nz, 8 * GRAD)
-        for n in inward:
-            if n in BY_Z:
-                sent(col_out.at[n], ns, 8 * n + 1)
-            else:
-                sent(row_out.at[n], nz, 8 * n + 1)
+        sent(row_out.at[LEFT], nz, 8 * LEFT + 1)
+        sent(col_out.at[RIGHT], ns, 8 * RIGHT + 1)
+        sent(grad_cell, hidden, 8 * GRAD)
 
 
 def to_hbm(upd, gpair, upd_hbm, gpair_hbm, sem):
@@ -713,20 +646,21 @@
             pltpu.VMEM((hidden, CELLS), F32),
             pltpu.VMEM((chans, CELLS), BF16),
             pltpu.VMEM((QUADS, 16 * nz, 128), F32),
-            pltpu.VMEM((6, ns, nz, CELLS), BF16),
-            pltpu.VMEM((6, ns, nz, CELLS), BF16),
-            pltpu.VMEM((6, nz, 16, width), BF16),
-            pltpu.VMEM((6, nz, 16, width), BF16),
+            pltpu.VMEM((2, ns, nz, CELLS), BF16),
+            pltpu.VMEM((2, ns, nz, CELLS), BF16),
+            pltpu.VMEM((2, nz, 16, width), BF16),
             pltpu.VMEM((3, nd, 16, width), BF16),
-            pltpu.VMEM((3, nd, 16, width), BF16),
-            pltpu.VMEM((6, nz, ns, CELLS), BF16),
-            pltpu.VMEM((6, nz, ns, CELLS), BF16),
-            pltpu.VMEM((6, ns, nz, CELLS), BF16),
-            pltpu.VMEM((6, ns, nz, CELLS), BF16),
-            pltpu.VMEM((6, 4 * ns, nz, CELLS), BF16),
-            pltpu.VMEM((2, ns * nz, QUADS, 128), BF16),
-            pltpu.VMEM((2, nd * ns, QUADS, 128), BF16),
-            pltpu.VMEM((ns // 4, nd * 16, 128), F32),
+            pltpu.VMEM((2, nz, ns, CELLS), BF16),
+            pltpu.VMEM((2, nz, ns, CELLS), BF16),
+            pltpu.VMEM((2, ns, nz, CELLS), BF16),
+            pltpu.VMEM((2, 4 * ns, nz, CELLS), BF16),
+            pltpu.VMEM((ns * nz, 1, QUADS, 128), BF16),
+            pltpu.VMEM((nd * ns, 1, QUADS, 128), BF16),
+            pltpu.VMEM((ns * nz, QUADS, 128), BF16),
+            pltpu.VMEM((nd * ns, QUADS, 128), BF16),
+            pltpu.VMEM((ns * nz, 2, QUADS, 128), BF16),
+            pltpu.VMEM((nd * ns, 2, QUADS, 128), BF16),
+            pltpu.VMEM((2, ns // 4, nd * 16, 128), F32),
             pltpu.VMEM((QUADS * ns * nz, 128), F32),
             pltpu.SemaphoreType.DMA((6,)),
             pltpu.SemaphoreType.DMA((48,)),

time: 64.9 us -> 64.7 us (level)
  no operation moved by 1% of the time
where the time goes in v5:
time: 64.7 us; the launch traced here: 64.6 us
  Pallas kernels  63.9 us (99%)
    pallas_call x1, Pallas kernels, on_device(): pl.pallas_call(functools.partial(kernel, nd, ns), out_shape=(shape, shape...  63.2 us

profile of v5, /device:TPU:1, one launch (start us, length us, event | category | flops | bytes accessed | tf_op | source)
XLA Modules:
  0.0 64.6 jit_solution(16299810713287973399)
XLA Ops:
  0.6 63.2 %shard_map.77 = (bf16[15,30,128]{2,1,0:T(8,128)(2,1)S(1)}, bf16[15,30,128]{2,1,0:T(8,128)(2,1)S(1)}) custom-call(bf16[15,30,128]{2,1,0:T(8,128)(2,1)} %x_hbm.1, bf16[15,30,128]{2,1,0:T(8,128)(2,1)} %cot_hbm.1, s32[1,480]{1,0:T(1,128)} %bitcast.1, bf16[128,512]{1,0:T(8,128)(2,1)} %wp_hbm.1, bf16[128,128]{1,0:T(8,128)(2,1)} %wg_hbm.1, bf16[128,128]{1,0:T(8,128)(2,1)} %wo_hbm.1), custom_call_target="tpu_custom_call" | custom-call | tf_op jit(solution)/shard_map/pallas_call | solution.py:633
  63.8 0.7 %shard_map.78 = (bf16[15,30,128]{2,1,0:T(8,128)(2,1)}, bf16[15,30,128]{2,1,0:T(8,128)(2,1)}) custom-call(bf16[15,30,128]{2,1,0:T(8,128)(2,1)S(1)} %get-tuple-element.4.upd, bf16[15,30,128]{2,1,0:T(8,128)(2,1)S(1)} %get-tuple-element.5.gpair), custom_call_target="tpu_custom_call" | custom-call | tf_op jit(solution)/shard_map/pallas_call | solution.py:673

commit v6 on v5

--- a/solution.py
+++ b/solution.py
@@ -319,15 +319,21 @@
     many = nd * 16
     tiles = ns // 4
 
+    hz = nz // 2
+    my_half = my_z // hz
+    run = 2 * hz
+
     def multiply(a, b, contract, k, h):
         right = own_in[b].reshape(many, width)
-        if contract[0][0] == 1:
-            part = own_in[a, pl.ds(h * nd // 2, nd // 2)].reshape(many // 2, width)
-        else:
-            part = own_in[a, :, :, pl.ds(h * width // 2, width // 2)].reshape(many, width // 2)
-        value = dot(part, right, contract)
-        for t in range(tiles):
-            own_mid[k, t, pl.ds(h * many // 2, many // 2), :] = value[:, t * 128 : t * 128 + 128]
+        for x in range(2):
+            first = (2 * x + h) * run
+            if contract[0][0] == 1:
+                part = own_in[a, pl.ds(first, run)].reshape(16 * run, width)
+            else:
+                part = own_in[a, :, :, pl.ds(16 * first, 16 * run)].reshape(many, 16 * run)
+            value = dot(part, right, contract)
+            for t in range(tiles):
+                own_mid[k, t, pl.ds(16 * first, 16 * run), :] = value[:, t * 128 : t * 128 + 128]
 
     my_tile = me_s // 4
     me = me_d * ns + me_s
@@ -336,14 +342,20 @@
         shift = jnp.where(lax.rem(step, 2) == 1, -((step + 1) // 2), step // 2)
         return lax.rem(my_tile + tiles // 2 + shift, tiles)
 
+    def half_pairs(h):
+        return [x * nz + h * hz + z for x in range(2) for z in range(hz)]
+
     def tiles_back(own, cell, sem, h, kinds, whole):
         mine = me_s * nz + my_z
+        turn = jnp.where(my_half == h, 0, hz // 2)
+        zs = [h * hz + lax.rem(my_z + r + turn, hz) for r in ring_order(hz)]
+        places = [(x, z) for z in zs for x in (other_x, my_x)]
 
         @pl.loop(0, tiles)
         def _(step):
             t = tile_at(step)
             for k in kinds:
-                for p in range(h * nz, h * nz + nz):
+                for p in half_pairs(h):
                     moved = swap_blocks(
                         [own_mid[k, t, pl.ds(32 * p + b, 8, stride=4), :] for b in range(4)]
                     )
@@ -351,9 +363,9 @@
                         line = moved[a].astype(BF16)
                         for core in range(2):
                             own[(2 * p + core) * ns + 4 * t + a, k] = line[4 * core : 4 * core + 4]
-            for n, z in enumerate(z_order):
+            for n, (x, z) in enumerate(places):
                 for core in range(2):
-                    d = at_dap(h, z, core)
+                    d = at_dap(x, z, core)
                     for a in range(4):
                         s = 4 * t + a
 
@@ -403,7 +415,7 @@
                     grad_own.at[me],
                     8 * n,
                     {"dap": owner_of(z, s), "ch": s},
-                    ARRIVALS + 4 * my_x + my_tile,
+                    ARRIVALS + 4 * my_half + my_tile,
                 ).start()
 
             if dz or dy or dx:
@@ -424,10 +436,10 @@
                 some = grad_own.at[pl.ds(0, count)]
                 push(some, some, 8 * GRAD, {"dap": me_d}, ARRIVALS + 4 * h + t).wait_recv()
 
-            mine_too = jnp.logical_and(t == my_tile, my_x == h)
+            mine_too = jnp.logical_and(t == my_tile, my_half == h)
             pl.when(mine_too)(lambda: arrived(2 * nd - 1))
             pl.when(jnp.logical_not(mine_too))(lambda: arrived(2 * nd))
-            for p in range(h * nz, h * nz + nz):
+            for p in half_pairs(h):
                 got = [
                     jnp.concatenate(
                         [
@@ -441,7 +453,7 @@
                 for b, rows in enumerate(swap_blocks(got)):
                     own_mid[0, t, pl.ds(32 * p + b, 8, stride=4), :] = rows
             lanes = pl.ds(pl.multiple_of(t * 128, 128), 128)
-            for d in range(h * nd // 2, (h + 1) * nd // 2):
+            for d in [2 * p + core for p in half_pairs(h) for core in range(2)]:
                 own_in[a, d, :, lanes] = own_mid[0, t, pl.ds(16 * d, 16), :].astype(BF16)
 
     lane = lax.broadcasted_iota(jnp.int32, (1, CELLS), 1)
@@ -561,11 +573,11 @@
         multiply(2, 1, ((1,), (0,)), 0, 0)
         tiles_back(grads_own, grads_cell, 8 * GRADS, 0, (0,), False)
         tiles_gathered(2, 1)
+        multiply(2, 0, ((0,), (0,)), 1, 0)
+        tiles_back(grads_own, grads_cell, 8 * GRADS, 0, (1,), False)
         multiply(2, 1, ((1,), (0,)), 0, 1)
         multiply(2, 0, ((0,), (0,)), 1, 1)
         tiles_back(grads_own, grads_cell, 8 * GRADS, 1, (0, 1), True)
-        multiply(2, 0, ((0,), (0,)), 1, 0)
-        tiles_back(grads_own, grads_cell, 8 * GRADS, 0, (1,), False)
         grads_cell[me_s * nz + my_z] = grads_own[me]
 
     base = dot(wg_ref[...], glogit[...], ((1,), (0,)))

time: 64.7 us -> 62.6 us (0.968)
  Pallas kernels: 63.9 us -> 61.8 us
    pallas_call x1, Pallas kernels: 63.2 us -> 61.1 us  [on_device(): pl.pallas_call(functools.partial(kernel, nd, ns), out_shape=(shape, shape...]
where the time goes in v6:
time: 62.6 us; the launch traced here: 62.5 us
  Pallas kernels  61.8 us (99%)
  between operations  0.64 us (1%)
    pallas_call x1, Pallas kernels, on_device(): pl.pallas_call(functools.partial(kernel, nd, ns), out_shape=(shape, shape...  61.1 us

profile of v6, /device:TPU:1, one launch (start us, length us, event | category | flops | bytes accessed | tf_op | source)
XLA Modules:
  0.0 62.5 jit_solution(11232942165059672968)
XLA Ops:
  0.6 61.1 %shard_map.77 = (bf16[15,30,128]{2,1,0:T(8,128)(2,1)S(1)}, bf16[15,30,128]{2,1,0:T(8,128)(2,1)S(1)}) custom-call(bf16[15,30,128]{2,1,0:T(8,128)(2,1)} %x_hbm.1, bf16[15,30,128]{2,1,0:T(8,128)(2,1)} %cot_hbm.1, s32[1,480]{1,0:T(1,128)} %bitcast.1, bf16[128,512]{1,0:T(8,128)(2,1)} %wp_hbm.1, bf16[128,128]{1,0:T(8,128)(2,1)} %wg_hbm.1, bf16[128,128]{1,0:T(8,128)(2,1)} %wo_hbm.1), custom_call_target="tpu_custom_call" | custom-call | tf_op jit(solution)/shard_map/pallas_call | solution.py:645
  61.8 0.7 %shard_map.78 = (bf16[15,30,128]{2,1,0:T(8,128)(2,1)}, bf16[15,30,128]{2,1,0:T(8,128)(2,1)}) custom-call(bf16[15,30,128]{2,1,0:T(8,128)(2,1)S(1)} %get-tuple-element.4.upd, bf16[15,30,128]{2,1,0:T(8,128)(2,1)S(1)} %get-tuple-element.5.gpair), custom_call_target="tpu_custom_call" | custom-call | tf_op jit(solution)/shard_map/pallas_call | solution.py:685

commit v7 on v6

--- a/solution.py
+++ b/solution.py
@@ -325,15 +325,17 @@
 
     def multiply(a, b, contract, k, h):
         right = own_in[b].reshape(many, width)
-        for x in range(2):
-            first = (2 * x + h) * run
-            if contract[0][0] == 1:
-                part = own_in[a, pl.ds(first, run)].reshape(16 * run, width)
-            else:
-                part = own_in[a, :, :, pl.ds(16 * first, 16 * run)].reshape(many, 16 * run)
-            value = dot(part, right, contract)
+        firsts = [(2 * x + h) * run for x in range(2)]
+        if contract[0][0] == 1:
+            parts = [own_in[a, pl.ds(f, run)].reshape(16 * run, width) for f in firsts]
+        else:
+            parts = [own_in[a, :, :, pl.ds(16 * f, 16 * run)].reshape(many, 16 * run) for f in firsts]
+        value = dot(jnp.concatenate(parts, axis=1 - contract[0][0]), right, contract)
+        for x, f in enumerate(firsts):
             for t in range(tiles):
-                own_mid[k, t, pl.ds(16 * first, 16 * run), :] = value[:, t * 128 : t * 128 + 128]
+                own_mid[k, t, pl.ds(16 * f, 16 * run), :] = value[
+                    16 * run * x : 16 * run * (x + 1), t * 128 : t * 128 + 128
+                ]
 
     my_tile = me_s // 4
     me = me_d * ns + me_s

time: 62.6 us -> 62.5 us (level)
  no operation moved by 1% of the time
where the time goes in v7:
time: 62.5 us; the launch traced here: 62.3 us
  Pallas kernels  61.7 us (99%)
  between operations  0.64 us (1%)
    pallas_call x1, Pallas kernels, on_device(): pl.pallas_call(functools.partial(kernel, nd, ns), out_shape=(shape, shape...  61 us

profile of v7, /device:TPU:1, one launch (start us, length us, event | category | flops | bytes accessed | tf_op | source)
XLA Modules:
  0.0 62.3 jit_solution(14369919738050859887)
XLA Ops:
  0.6 61.0 %shard_map.77 = (bf16[15,30,128]{2,1,0:T(8,128)(2,1)S(1)}, bf16[15,30,128]{2,1,0:T(8,128)(2,1)S(1)}) custom-call(bf16[15,30,128]{2,1,0:T(8,128)(2,1)} %x_hbm.1, bf16[15,30,128]{2,1,0:T(8,128)(2,1)} %cot_hbm.1, s32[1,480]{1,0:T(1,128)} %bitcast.1, bf16[128,512]{1,0:T(8,128)(2,1)} %wp_hbm.1, bf16[128,128]{1,0:T(8,128)(2,1)} %wg_hbm.1, bf16[128,128]{1,0:T(8,128)(2,1)} %wo_hbm.1), custom_call_target="tpu_custom_call" | custom-call | tf_op jit(solution)/shard_map/pallas_call | solution.py:647
  61.6 0.7 %shard_map.78 = (bf16[15,30,128]{2,1,0:T(8,128)(2,1)}, bf16[15,30,128]{2,1,0:T(8,128)(2,1)}) custom-call(bf16[15,30,128]{2,1,0:T(8,128)(2,1)S(1)} %get-tuple-element.4.upd, bf16[15,30,128]{2,1,0:T(8,128)(2,1)S(1)} %get-tuple-element.5.gpair), custom_call_target="tpu_custom_call" | custom-call | tf_op jit(solution)/shard_map/pallas_call | solution.py:687
